TPU v7x, 128 devices: a whole 4x4x4 slice. The times are simulated.
128 devices in a mesh: dp: 16 (over y_hi, z, core), mp: 8 (over y_lo, x).
Axes of the slice: x: 4, y: 4 (y_hi: 2, y_lo: 2; y = y_hi * 2 + y_lo), z: 4, core: 2. Of those that a mesh axis runs over, the one named last changes fastest.
Arguments:
- features: bfloat16 [16384, 8192], P('dp', 'mp'), may hold values from -6 to 6
- v_weight: bfloat16 [3, 8192, 1024], P(None, 'mp', 'dp'), may hold values from -0.0625 to 0.0625
- u_weight: bfloat16 [3, 1024, 8192], P(None, 'dp', 'mp'), may hold values from -0.1875 to 0.1875
- cross_bias: float32 [3, 8192], P(None, 'mp'), may hold values from -3 to 3
Outputs:
- crossed: bfloat16 [16384, 8192], P('dp', 'mp')
All inputs are finite; a program needn't handle non-finite values.
Results may differ from a plain program's by a relative error of at most 0.009.
Values may be sent and summed in bfloat16 or wider, within the bound.
A program may use at most 64 MiB of HBM per device.

v0:
```python
import jax
import jax.numpy as jnp
from jax import lax
from jax.sharding import PartitionSpec as P


def split_up(array, dim, length):
    dims = array.shape
    blocks = array.reshape(*dims[:dim], length, dims[dim] // length, *dims[dim + 1 :])
    return jnp.moveaxis(blocks, dim, 0)


def sum_at_owner(array, axis, dim):
    blocks = split_up(array, dim, lax.axis_size(axis))
    arrived = lax.all_to_all(blocks, axis, split_axis=0, concat_axis=0, tiled=True)
    return arrived.sum(axis=0)


def joined_along(blocks, dim):
    dims = list(blocks.shape[1:])
    dims[dim] *= blocks.shape[0]
    return jnp.moveaxis(blocks, 0, dim).reshape(dims)


def sent_to_all(array, axis):
    length = lax.axis_size(axis)
    return lax.all_to_all(
        jnp.broadcast_to(array[None], (length, *array.shape)), axis, 0, 0, tiled=True
    )


def collect(array, axis, dim):
    return joined_along(sent_to_all(array, axis), dim)


def local(features, v_weight, u_weight, cross_bias):
    carried = features
    layers = v_weight.shape[0]
    v_whole = lax.all_gather(v_weight, "dp", axis=2, tiled=True)
    u_whole = lax.all_gather(u_weight, "dp", axis=1, tiled=True)
    for layer_number in range(layers):
        current = carried
        partial_value = jnp.dot(current, v_whole[layer_number], preferred_element_type=jnp.float32)
        scattered = sum_at_owner(partial_value, "mp", 1).astype(jnp.bfloat16)
        rank_proj = collect(scattered, "mp", 1)
        cross_term = jnp.dot(rank_proj, u_whole[layer_number], preferred_element_type=jnp.float32)
        cross_term = cross_term + cross_bias[layer_number]
        carried = (features.astype(jnp.float32) * cross_term + current.astype(jnp.float32)).astype(
            jnp.bfloat16
        )
    return carried


def solution(mesh):
    return jax.shard_map(
        local,
        mesh=mesh,
        in_specs=(P("dp", "mp"), P(None, "mp", "dp"), P(None, "dp", "mp"), P(None, "mp")),
        out_specs=P("dp", "mp"),
        check_vma=False,
    )
```

profile of v0, /device:TPU:0, one launch (start us, length us, event | category | flops | bytes accessed | tf_op | source)
XLA Modules:
  0.0 390.2 jit_solution(2678584646488441746)
XLA Ops:
  6.5 0.0 all-gather.3.cloned.1.call-start
  6.5 0.7 all-gather.3.cloned.1.call-update
  7.3 0.0 all-gather.5.cloned.1.call-start
  7.3 0.7 all-gather.5.cloned.1.call-update
  8.0 0.0 copy-start.3
  8.0 68.2 %all-gather.3.cloned.1.call-done = bf16[3,1024,1024]{1,2,0:T(8,128)(2,1)} async-done(((bf16[3,1024,64]{1,2,0:T(8,128)(2,1)}), bf16[3,1024,1024]{1,2,0:T(8,128)(2,1)}) %all-gather.3.cloned.1.call-update) | async-done | bytes 6291472 | tf_op jit(solution)/shard_map/all_gather | solution.py:39
  76.2 5.6 %fusion.11 = (bf16[1,1024,1024]{1,2,0:T(8,128)(2,1)}, bf16[1,1024,1024]{1,2,0:T(8,128)(2,1)}, bf16[1,1024,1024]{1,2,0:T(8,128)(2,1)S(1)}) fusion(bf16[3,1024,1024]{1,2,0:T(8,128)(2,1)} %all-gather.3.cloned.1.call-done), kind=kLoop, calls=%fused_computation.21 | loop fusion | bytes 12582912 | tf_op jit(solution)/shard_map/slice | solution.py:43
  81.8 0.0 copy-done.3
  81.8 2.4 convolution_bitcast_fusion.2
  84.2 54.2 %all_to_all.30 = f32[8,1024,128]{2,1,0:T(8,128)} all-to-all(f32[8,1024,128]{2,1,0:T(8,128)S(1)} %convolution_bitcast_fusion.2), channel_id=1, replica_groups=mesh['dp'=16,'mp'=8] {'mp'}, dimensions={0} | all-to-all | bytes 8388608 | tf_op jit(solution)/shard_map/all_to_all | solution.py:15
  138.4 2.4 reduce_sum.27
  140.8 0.1 copy.5
  140.9 1.6 broadcast_in_dim.6
  142.5 0.0 copy-start.2
  142.5 4.4 %all-to-all-start.1 = ((bf16[8,1024,128]{1,2,0:T(8,128)(2,1)}), bf16[8,1024,128]{1,2,0:T(8,128)(2,1)S(1)}, u32[]{:S(2)}, u32[]{:S(2)}) async-start(bf16[8,1024,128]{1,2,0:T(8,128)(2,1)} %broadcast_in_dim.6), calls=%async_computation.1 | async-start | bytes 4194304 | tf_op jit(solution)/shard_map/all_to_all | solution.py:27
  146.9 0.0 copy-done.2
  146.9 46.3 %all-gather.5.cloned.1.call-done = bf16[3,1024,1024]{2,1,0:T(8,128)(2,1)} async-done(((bf16[3,64,1024]{2,1,0:T(8,128)(2,1)}), bf16[3,1024,1024]{2,1,0:T(8,128)(2,1)}) %all-gather.5.cloned.1.call-update) | async-done | bytes 6291472 | tf_op jit(solution)/shard_map/all_gather | solution.py:40
  193.3 0.0 all-to-all-done.1
  193.3 0.0 copy-start.1
  193.3 5.1 %fusion = bf16[1024,1024]{1,0:T(8,128)(2,1)S(1)} fusion(bf16[1024,1024]{1,0:T(8,128)(2,1)} %param.4, f32[1024]{0:T(1024)S(1)} %bitcast.71, bf16[1024,1024]{0,1:T(8,128)(2,1)S(1)} %bitcast.63, bf16[3,1024,1024]{2,1,0:T(8,128)(2,1)} %all-gather.5.cloned.1.call-done), kind=kOutput, calls=%fused_computation.4 | convolution fusion | flops 2152726528 | bytes 8392704 | tf_op jit(solution)/shard_map/dot_general | solution.py:46
  198.3 0.0 copy-start.8
  198.4 0.0 copy-done.1
  198.4 2.4 convolution_bitcast_fusion.1
  200.7 0.0 copy-done.8
  200.8 54.0 %all_to_all.31 = f32[8,1024,128]{2,1,0:T(8,128)} all-to-all(f32[8,1024,128]{2,1,0:T(8,128)S(1)} %convolution_bitcast_fusion.1), channel_id=1, replica_groups=mesh['dp'=16,'mp'=8] {'mp'}, dimensions={0} | all-to-all | bytes 8388608 | tf_op jit(solution)/shard_map/all_to_all | solution.py:15
  254.8 2.4 reduce_sum.28
  257.2 0.1 copy.6
  257.3 0.3 broadcast_in_dim.7
  257.6 0.0 copy-start.4
  257.6 0.0 copy-start.9
  257.6 29.8 %all_to_all.32 = bf16[8,1024,128]{1,2,0:T(8,128)(2,1)S(1)} all-to-all(bf16[8,1024,128]{1,2,0:T(8,128)(2,1)S(1)} %broadcast_in_dim.7), channel_id=1, replica_groups=mesh['dp'=16,'mp'=8] {'mp'}, dimensions={0} | all-to-all | bytes 4194304 | tf_op jit(solution)/shard_map/all_to_all | solution.py:27
  287.4 0.0 copy-done.4
  287.4 0.0 copy-done.9
  287.4 4.6 %fusion.2 = bf16[1024,1024]{1,0:T(8,128)(2,1)S(1)} fusion(bf16[1024,1024]{1,0:T(8,128)(2,1)S(1)} %copy-done.4, bf16[1024,1024]{1,0:T(8,128)(2,1)S(1)} %copy-done.9, f32[1024]{0:T(1024)S(1)} %bitcast.70, bf16[1024,1024]{0,1:T(8,128)(2,1)S(1)} %bitcast.65, bf16[3,1024,1024]{2,1,0:T(8,128)(2,1)} %all-gather.5.cloned.1.call-done), kind=kOutput, calls=%fused_computation.6 | convolution fusion | flops 2153775104 | bytes 10489856 | tf_op jit(solution)/shard_map/dot_general | solution.py:46
  292.0 0.0 copy-start.6
  292.0 0.0 copy-done
  292.0 2.4 convolution_bitcast_fusion
  294.4 0.0 copy-done.6
  294.4 51.9 %all_to_all.33 = f32[8,1024,128]{2,1,0:T(8,128)} all-to-all(f32[8,1024,128]{2,1,0:T(8,128)S(1)} %convolution_bitcast_fusion), channel_id=1, replica_groups=mesh['dp'=16,'mp'=8] {'mp'}, dimensions={0} | all-to-all | bytes 8388608 | tf_op jit(solution)/shard_map/all_to_all | solution.py:15
  346.3 2.4 reduce_sum.29
  348.7 0.1 copy.7
  348.9 0.3 broadcast_in_dim.8
  349.1 0.0 copy-start.5
  349.1 0.0 copy-start.7
  349.1 28.5 %all_to_all.34 = bf16[8,1024,128]{1,2,0:T(8,128)(2,1)S(1)} all-to-all(bf16[8,1024,128]{1,2,0:T(8,128)(2,1)S(1)} %broadcast_in_dim.8), channel_id=1, replica_groups=mesh['dp'=16,'mp'=8] {'mp'}, dimensions={0} | all-to-all | bytes 4194304 | tf_op jit(solution)/shard_map/all_to_all | solution.py:27
  377.7 0.0 copy-done.5
  377.7 0.0 copy-done.7
  377.7 5.7 %fusion.4 = bf16[1024,1024]{1,0:T(8,128)(2,1)} fusion(bf16[1024,1024]{1,0:T(8,128)(2,1)S(1)} %copy-done.5, bf16[1024,1024]{1,0:T(8,128)(2,1)S(1)} %copy-done.7, f32[1024]{0:T(1024)S(1)} %bitcast.69, bf16[1024,1024]{0,1:T(8,128)(2,1)S(1)} %bitcast.64, bf16[3,1024,1024]{2,1,0:T(8,128)(2,1)} %all-gather.5.cloned.1.call-done), kind=kOutput, calls=%fused_computation.8 | convolution fusion | flops 2153775104 | bytes 10489856 | tf_op jit(solution)/shard_map/dot_general | solution.py:46
  (2 shorter events, 0.0 us)
Async XLA Ops:
  6.5 69.7 %all-gather.3.cloned.1.call-start = ((), (), s32[]{:S(2)}) async-start(), calls=%async_computation.6 | async-start | bytes 6684672 | tf_op jit(solution)/shard_map/all_gather | solution.py:39
  7.3 186.0 %all-gather.5.cloned.1.call-start = ((), (), s32[]{:S(2)}) async-start(), calls=%async_computation.7 | async-start | bytes 6684672 | tf_op jit(solution)/shard_map/all_gather | solution.py:40
  8.0 73.8 %copy-start.3 = (bf16[1024,1024]{1,0:T(8,128)(2,1)S(1)}, bf16[1024,1024]{1,0:T(8,128)(2,1)}, u32[]{:S(2)}) copy-start(bf16[1024,1024]{1,0:T(8,128)(2,1)} %param.4) | copy-start | bytes 6291460
  142.5 4.4 %copy-start.2 = (f32[3,1024]{1,0:T(4,128)S(1)}, f32[3,1024]{1,0:T(4,128)}, u32[]{:S(2)}) copy-start(f32[3,1024]{1,0:T(4,128)} %param.7) | copy-start | bytes 36868
  142.5 50.8 %all-to-all-start.1 = ((bf16[8,1024,128]{1,2,0:T(8,128)(2,1)}), bf16[8,1024,128]{1,2,0:T(8,128)(2,1)S(1)}, u32[]{:S(2)}, u32[]{:S(2)}) async-start(bf16[8,1024,128]{1,2,0:T(8,128)(2,1)} %broadcast_in_dim.6), calls=%async_computation.1 | async-start | bytes 4194304 | tf_op jit(solution)/shard_map/all_to_all | solution.py:27
  193.3 5.1 %copy-start.1 = (bf16[1,1024,1024]{1,2,0:T(8,128)(2,1)S(1)}, bf16[1,1024,1024]{1,2,0:T(8,128)(2,1)}, u32[]{:S(2)}) copy-start(bf16[1,1024,1024]{1,2,0:T(8,128)(2,1)} %get-tuple-element.6) | copy-start | bytes 6291460
  198.3 2.4 copy-start.8
  257.6 29.8 %copy-start.4 = (bf16[1024,1024]{1,0:T(8,128)(2,1)S(1)}, bf16[1024,1024]{1,0:T(8,128)(2,1)}, u32[]{:S(2)}) copy-start(bf16[1024,1024]{1,0:T(8,128)(2,1)} %param.4) | copy-start | bytes 6291460
  257.6 29.8 %copy-start.9 = (bf16[1024,1024]{1,0:T(8,128)(2,1)S(1)}, bf16[1024,1024]{1,0:T(8,128)(2,1)}, u32[]{:S(2)}) copy-start(bf16[1024,1024]{1,0:T(8,128)(2,1)} %copy-done.8) | copy-start | bytes 6291460
  287.4 4.6 %copy-start = (bf16[1,1024,1024]{1,2,0:T(8,128)(2,1)S(1)}, bf16[1,1024,1024]{1,2,0:T(8,128)(2,1)}, u32[]{:S(2)}) copy-start(bf16[1,1024,1024]{1,2,0:T(8,128)(2,1)} %get-tuple-element.5) | copy-start | bytes 6291460
  292.0 2.4 copy-start.6
  349.1 28.5 %copy-start.5 = (bf16[1024,1024]{1,0:T(8,128)(2,1)S(1)}, bf16[1024,1024]{1,0:T(8,128)(2,1)}, u32[]{:S(2)}) copy-start(bf16[1024,1024]{1,0:T(8,128)(2,1)} %param.4) | copy-start | bytes 6291460
  349.1 28.5 %copy-start.7 = (bf16[1024,1024]{1,0:T(8,128)(2,1)S(1)}, bf16[1024,1024]{1,0:T(8,128)(2,1)}, u32[]{:S(2)}) copy-start(bf16[1024,1024]{1,0:T(8,128)(2,1)} %copy-done.6) | copy-start | bytes 6291460
Sparse Core Ops, SparseCore 0:
  9.9 66.3 all-gather.2
  78.7 114.4 all-gather.4
where the time goes:
time: 391 us; the launch traced here: 390 us
  blocking collectives  218 us (56%)
  waiting for transfers between devices  116 us (30%)
  matrix products  22.5 us (6%)
  between operations  13.6 us (3%)
  local copies, waits for them, and re-layouts  8.19 us (2%)
  other arithmetic  7.21 us (2%)
  starting transfers between devices  4.43 us (1%)
    all_to_all x3, blocking collectives, sum_at_owner(): lax.all_to_all(blocks, axis, split_axis=0, concat_axis=0, tiled=True)  160 us
    all_gather x1, waiting for transfers between devices, local(): v_whole = lax.all_gather(v_weight, 'dp', axis=2, tiled=True)  68.2 us
    all_to_all x2, blocking collectives, sent_to_all(): lax.all_to_all(jnp.broadcast_to(array[None], (length, *array.shape)), axi...  58.3 us
    all_gather x1, waiting for transfers between devices, local(): u_whole = lax.all_gather(u_weight, 'dp', axis=1, tiled=True)  46.3 us
    dot_general x3, matrix products, local(): jnp.dot(rank_proj, u_whole[layer_number], preferred_element_type=jnp.floa...  15.4 us
  transfers between devices with their start and end apart: 3, of which 2 were waited for; matrix products, arithmetic and copies ran while one was open for 3% of the time, Pallas kernels for 0%

commit v1 on v0

v1 whole, which is shorter than its diff:
```python
import jax
import jax.numpy as jnp
from jax import lax
from jax.experimental import pallas as pl
from jax.experimental.pallas import tpu as pltpu
from jax.sharding import PartitionSpec as P

MESH = pl.DeviceIdType.MESH
BF16 = jnp.bfloat16
F32 = jnp.float32

CHUNKS = 8
LAG = (0, 1, 2, 3, 4, 5)


def kernel(
    f_ref, v_ref, u_ref, b_ref, out_ref,
    vbuf, v_full, u_full, carried, part, rank, rs1, s2, rs2, ysend, yrecv,
    ss, rs, wss, wrs, w0s, w0r,
):
    layers = v_ref.shape[0]
    rows = f_ref.shape[0] // CHUNKS
    half = rows // 2
    depth = f_ref.shape[1]
    feat_half = depth // 2
    share = u_ref.shape[1]
    block_width = 2 * share
    tasks = layers * CHUNKS
    quarter = v_full.shape[2] // 4

    dp, mp = lax.axis_index("dp"), lax.axis_index("mp")
    y_hi, z, core = dp // 8, lax.rem(dp // 2, 4), lax.rem(dp, 2)
    y_lo, x = mp // 4, lax.rem(mp, 4)
    xr, xl, xo = lax.rem(x + 1, 4), lax.rem(x + 3, 4), lax.rem(x + 2, 4)
    zr, zl, zo = lax.rem(z + 1, 4), lax.rem(z + 3, 4), lax.rem(z + 2, 4)

    def at(y_hi=y_hi, z=z, core=core, y_lo=y_lo, x=x):
        return ((y_hi * 4 + z) * 2 + core, y_lo * 4 + x)

    right, left, across = at(x=xr), at(x=xl), at(y_lo=1 - y_lo)
    z_right, z_left, y_far, partner = at(z=zr), at(z=zl), at(y_hi=1 - y_hi), at(core=1 - core)

    barrier = pltpu.get_barrier_semaphore()
    for device in (right, left, across, z_right, z_left, y_far, partner):
        pl.semaphore_signal(barrier, inc=1, device_id=device, device_id_type=MESH)
    pl.semaphore_wait(barrier, 7)

    def send(src, dst, send_sem, recv_sem, device):
        return pltpu.make_async_remote_copy(
            src_ref=src, dst_ref=dst, send_sem=send_sem, recv_sem=recv_sem,
            device_id=device, device_id_type=MESH,
        )

    own = y_hi * 4 + z
    same = y_hi * 4
    other = (1 - y_hi) * 4

    def piece(matrix, block):
        layer = matrix // 2
        if matrix % 2 == 0:
            return v_full.at[
                layer,
                pl.ds(pl.multiple_of(core * feat_half, feat_half), feat_half),
                pl.ds(pl.multiple_of(block * block_width, block_width), block_width),
            ]
        return u_full.at[layer, pl.ds(pl.multiple_of(block * block_width + core * share, share), share), :]

    def move(matrix, block, number, device):
        ref = piece(matrix, block)
        return send(ref, ref, wss.at[matrix, number], wrs.at[matrix, number], device)

    def swap_v(layer):
        return send(v_ref.at[layer], vbuf.at[layer], w0s.at[layer], w0r.at[layer], partner)

    def swap_u(layer):
        place = u_full.at[layer, pl.ds(pl.multiple_of(own * block_width + core * share, share), share), :]
        return send(u_ref.at[layer], place, w0s.at[layers + layer], w0r.at[layers + layer], partner)

    def far(matrix):
        return [move(matrix, own, 0, y_far), move(matrix, own, 1, z_right), move(matrix, own, 2, z_left)]

    def near(matrix):
        block = other + z
        return [move(matrix, block, 3, z_right), move(matrix, block, 4, z_left), move(matrix, block, 7, partner)]

    def onward(matrix):
        return [
            move(matrix, same + zl, 5, z_right),
            move(matrix, other + zr, 6, z_left),
            move(matrix, same + zl, 8, partner),
            move(matrix, same + zr, 9, partner),
            move(matrix, other + zl, 10, partner),
            move(matrix, other + zr, 11, partner),
        ]

    def last(matrix):
        return [move(matrix, same + zo, 12, partner), move(matrix, other + zo, 13, partner)]

    def arrived(matrix, numbers):
        for number in numbers:
            move(matrix, own, number, partner).wait_recv()

    def start(copies):
        for copy in copies:
            copy.start()

    def weights_0(matrix):
        layer = matrix // 2
        if matrix % 2 == 0:
            swap_v(layer).wait_recv()
            mine, theirs = v_ref[layer], vbuf[layer]
            first = core == 0
            low = jnp.where(first, mine, theirs)
            high = jnp.where(first, theirs, mine)
            v_full[layer, :, pl.ds(pl.multiple_of(own * block_width, block_width), block_width)] = (
                jnp.concatenate([low, high], axis=1)
            )
        start(far(matrix))

    def weights_1(matrix):
        arrived(matrix, (0,))
        start(near(matrix))

    def weights_2(matrix):
        arrived(matrix, (1, 2, 3, 4))
        start(onward(matrix))

    def weights_3(matrix):
        arrived(matrix, (5, 6))
        start(last(matrix))

    def weights_4(matrix):
        arrived(matrix, (7, 8, 9, 10, 11, 12, 13))
        if matrix % 2 == 1:
            swap_u(matrix // 2).wait_recv()

    weight_stages = (weights_0, weights_1, weights_2, weights_3, weights_4)

    upper, lower = pl.ds(0, half), pl.ds(half, half)

    def first_hop(t):
        return [
            send(part.at[t, xo, upper], rs1.at[t, 0], ss.at[t, 0], rs.at[t, 0], right),
            send(part.at[t, xo, lower], rs1.at[t, 2], ss.at[t, 2], rs.at[t, 2], left),
            send(part.at[t, xr, lower], rs1.at[t, 1], ss.at[t, 1], rs.at[t, 1], right),
            send(part.at[t, xl, upper], rs1.at[t, 3], ss.at[t, 3], rs.at[t, 3], left),
        ]

    def second_hop(t):
        return [
            send(s2.at[t, 0], rs2.at[t, 0], ss.at[t, 4], rs.at[t, 4], right),
            send(s2.at[t, 1], rs2.at[t, 1], ss.at[t, 5], rs.at[t, 5], left),
        ]

    def exchange(t):
        return [send(ysend.at[t], yrecv.at[t], ss.at[t, 6], rs.at[t, 6], across)]

    def share_1(t):
        return [
            send(rank.at[t, x], rank.at[t, x], ss.at[t, 7], rs.at[t, 7], right),
            send(rank.at[t, x], rank.at[t, x], ss.at[t, 8], rs.at[t, 8], left),
        ]

    def share_2(t):
        return [
            send(rank.at[t, xl, upper], rank.at[t, xl, upper], ss.at[t, 9], rs.at[t, 9], right),
            send(rank.at[t, xr, lower], rank.at[t, xr, lower], ss.at[t, 10], rs.at[t, 10], left),
        ]

    def stage_0(t):
        layer, chunk = t // CHUNKS, lax.rem(t, CHUNKS)
        for q in range(4):
            part[t, q] = jnp.dot(
                carried[chunk], v_full[layer, :, q * quarter : (q + 1) * quarter], preferred_element_type=F32
            ).astype(BF16)
        start(first_hop(t))

    def stage_1(t):
        hop = first_hop(t)
        hop[0].wait_recv()
        s2[t, 0] = (part[t, xr, upper].astype(F32) + rs1[t, 0].astype(F32)).astype(BF16)
        hop[1].wait_recv()
        s2[t, 1] = (part[t, xl, lower].astype(F32) + rs1[t, 2].astype(F32)).astype(BF16)
        start(second_hop(t))

    def stage_2(t):
        hop = first_hop(t)
        hop[2].wait_recv()
        hop[3].wait_recv()
        for copy in second_hop(t):
            copy.wait_recv()
        ysend[t, upper] = (
            part[t, x, upper].astype(F32) + rs2[t, 0].astype(F32) + rs1[t, 3].astype(F32)
        ).astype(BF16)
        ysend[t, lower] = (
            part[t, x, lower].astype(F32) + rs2[t, 1].astype(F32) + rs1[t, 1].astype(F32)
        ).astype(BF16)
        start(exchange(t))

    def stage_3(t):
        exchange(t)[0].wait_recv()
        rank[t, x] = (ysend[t].astype(F32) + yrecv[t].astype(F32)).astype(BF16)
        start(share_1(t))

    def stage_4(t):
        for copy in share_1(t):
            copy.wait_recv()
        start(share_2(t))

    def stage_5(t):
        layer, chunk = t // CHUNKS, lax.rem(t, CHUNKS)
        for copy in share_2(t):
            copy.wait_recv()
        where = pl.ds(pl.multiple_of(chunk * rows, rows), rows)
        for j in range(4):
            columns = slice(j * depth // 4, (j + 1) * depth // 4)
            total = b_ref[layer][:, columns]
            for q in range(4):
                total = total + jnp.dot(
                    rank[t, q],
                    u_full[layer, q * quarter : (q + 1) * quarter, columns],
                    preferred_element_type=F32,
                )
            carried[chunk, :, columns] = (
                f_ref[where, columns].astype(F32) * total + carried[chunk, :, columns].astype(F32)
            ).astype(BF16)

        @pl.when(layer == layers - 1)
        def _():
            out_ref[where, :] = carried[chunk]

    for layer in range(layers):
        swap_v(layer).start()
    for layer in range(layers):
        swap_u(layer).start()
    for layer in range(layers):
        u_full[layer, pl.ds(pl.multiple_of(own * block_width + core * share, share), share), :] = u_ref[layer]
    weights_0(0)

    @pl.loop(0, CHUNKS)
    def _(chunk):
        carried[chunk] = f_ref[pl.ds(pl.multiple_of(chunk * rows, rows), rows), :]

    weights_1(0)
    weights_2(0)
    weights_3(0)
    weights_0(1)
    weights_1(1)
    weights_4(0)

    plan = {}
    for stage in range(2, 5):
        plan.setdefault(stage - 2, []).append((stage, 1))
    for matrix, begin in ((2, 2), (3, 6), (4, 9), (5, 13)):
        for stage in range(5):
            plan.setdefault(begin + stage, []).append((stage, matrix))

    @pl.loop(0, tasks + LAG[5])
    def _(i):
        for when, steps in sorted(plan.items()):
            @pl.when(i == when)
            def _(steps=steps):
                for stage, matrix in steps:
                    weight_stages[stage](matrix)

        for number, stage in ((4, stage_4), (3, stage_3), (2, stage_2), (1, stage_1), (5, stage_5), (0, stage_0)):
            t = i - LAG[number]

            @pl.when(jnp.logical_and(t >= 0, t < tasks))
            def _(stage=stage, t=t):
                stage(t)

    @pl.loop(0, tasks)
    def _(t):
        for copies in (first_hop, second_hop, exchange, share_1, share_2):
            for copy in copies(t):
                copy.wait_send()

    for layer in range(layers):
        swap_v(layer).wait_send()
        swap_u(layer).wait_send()
    for matrix in range(2 * layers):
        for copies in (far, near, onward, last):
            for copy in copies(matrix):
                copy.wait_send()


def local(features, v_weight, u_weight, cross_bias):
    layers, depth, share = v_weight.shape
    rank = share * lax.axis_size("dp")
    rows = features.shape[0] // CHUNKS
    half = rows // 2
    quarter = rank // 4
    tasks = layers * CHUNKS
    dma = pltpu.SemaphoreType.DMA
    vmem = pl.BlockSpec(memory_space=pltpu.VMEM)
    return pl.pallas_call(
        kernel,
        out_shape=jax.ShapeDtypeStruct(features.shape, BF16),
        in_specs=[vmem] * 4,
        out_specs=vmem,
        scratch_shapes=[
            pltpu.VMEM((layers, depth, share), BF16),
            pltpu.VMEM((layers, depth, rank), BF16),
            pltpu.VMEM((layers, rank, depth), BF16),
            pltpu.VMEM((CHUNKS, rows, depth), BF16),
            pltpu.VMEM((tasks, 4, rows, quarter), BF16),
            pltpu.VMEM((tasks, 4, rows, quarter), BF16),
            pltpu.VMEM((tasks, 4, half, quarter), BF16),
            pltpu.VMEM((tasks, 2, half, quarter), BF16),
            pltpu.VMEM((tasks, 2, half, quarter), BF16),
            pltpu.VMEM((tasks, rows, quarter), BF16),
            pltpu.VMEM((tasks, rows, quarter), BF16),
            dma((tasks, 11)),
            dma((tasks, 11)),
            dma((2 * layers, 14)),
            dma((2 * layers, 14)),
            dma((2 * layers,)),
            dma((2 * layers,)),
        ],
        compiler_params=pltpu.CompilerParams(
            collective_id=0, has_side_effects=True, vmem_limit_bytes=67043328
        ),
    )(features, v_weight, u_weight, cross_bias.reshape(layers, 1, depth))


def solution(mesh):
    return jax.shard_map(
        local,
        mesh=mesh,
        in_specs=(P("dp", "mp"), P(None, "mp", "dp"), P(None, "dp", "mp"), P(None, "mp")),
        out_specs=P("dp", "mp"),
        check_vma=False,
    )
```

time: 391 us -> 183 us (0.47)
  blocking collectives: 218 us -> 0 us
  Pallas kernels: 0 us -> 176 us
  waiting for transfers between devices: 116 us -> 0 us
  matrix products: 22.5 us -> 0 us
  between operations: 13.6 us -> 0.01 us
  other arithmetic: 7.21 us -> 0 us
  starting transfers between devices: 4.43 us -> 0 us
    all_to_all x5 -> x0, blocking collectives: 218 us -> none  [the longest x3 160 us: sum_at_owner(): lax.all_to_all(blocks, axis, split_axis=0, concat_axis=0, tiled=True)]
    pallas_call x0 -> x1, Pallas kernels: none -> 176 us  [local(): pl.pallas_call(kernel, out_shape=jax.ShapeDtypeStruct(features.shape, BF1...]
    all_gather x2 -> x0, waiting for transfers between devices: 115 us -> none  [the longest x1 68.2 us: local(): v_whole = lax.all_gather(v_weight, 'dp', axis=2, tiled=True)]
    dot_general x6 -> x0, matrix products: 22.5 us -> none  [the longest x3 15.4 us: local(): jnp.dot(rank_proj, u_whole[layer_number], preferred_element_type=jnp.floa...]
    reduce_sum x3 -> x0, other arithmetic: 7.21 us -> none  [sum_at_owner(): return arrived.sum(axis=0)]
    slice x2 -> x0, local copies, waits for them, and re-layouts: 5.59 us -> none  [the longest x1 5.58 us: local(): v_whole[layer_number]]
    unnamed x20 -> x2, local copies, waits for them, and re-layouts: 0.05 us -> 5.23 us
    all_to_all x1 -> x0, starting transfers between devices: 4.39 us -> none  [sent_to_all(): lax.all_to_all(jnp.broadcast_to(array[None], (length, *array.shape)), axi...]
  transfers between devices with their start and end apart: 3 -> 0, of which waited for: 2 -> 0; matrix products, arithmetic and copies ran while one was open for 3% -> 0% of each run, Pallas kernels for 0% -> 0%
where the time goes in v1:
time: 183 us
  Pallas kernels  176 us (96%)
  local copies, waits for them, and re-layouts  6.55 us (4%)
    pallas_call x1, Pallas kernels, local(): pl.pallas_call(kernel, out_shape=jax.ShapeDtypeStruct(features.shape, BF1...  176 us
    unnamed x2, local copies, waits for them, and re-layouts  5.23 us

profile of v1, /device:TPU:0, one launch (start us, length us, event | category | flops | bytes accessed | tf_op | source)
XLA Modules:
  0.0 182.7 jit_solution(5083157770227446377)
XLA Ops:
  0.0 1.3 reshape.3.b_ref
  1.3 2.2 %copy.5.v_ref = bf16[3,1024,64]{2,1,0:T(8,128)(2,1)} copy(bf16[3,1024,64]{1,2,0:T(8,128)(2,1)} %param.5) | data formatting | bytes 786432 | tf_op args[1]
  3.5 176.1 %shard_map.46 = bf16[1024,1024]{1,0:T(8,128)(2,1)} custom-call(bf16[1024,1024]{1,0:T(8,128)(2,1)} %f_ref.1, bf16[3,1024,64]{2,1,0:T(8,128)(2,1)} %copy.5.v_ref, bf16[3,64,1024]{2,1,0:T(8,128)(2,1)} %u_ref.1, f32[3,1,1024]{2,1,0:T(1,128)} %reshape.3.b_ref), custom_call_target="tpu_custom_call" | custom-call | tf_op jit(solution)/shard_map/pallas_call | solution.py:297
  179.6 3.1 %copy.7 = bf16[1024,1024]{1,0:T(8,128)(2,1)} copy(bf16[1024,1024]{1,0:T(8,128)(2,1)} %shard_map.46) | data formatting | bytes 4194304

commit v2 on v1

--- a/solution.py
+++ b/solution.py
@@ -15,18 +15,17 @@
 
 def kernel(
     f_ref, v_ref, u_ref, b_ref, out_ref,
-    vbuf, v_full, u_full, carried, part, rank, rs1, s2, rs2, ysend, yrecv,
-    ss, rs, wss, wrs, w0s, w0r,
+    w_full, carried, part, rank, rs1, s2, rs2, ysend, yrecv,
+    ss, rs, wss, wrs,
 ):
     layers = v_ref.shape[0]
     rows = f_ref.shape[0] // CHUNKS
     half = rows // 2
     depth = f_ref.shape[1]
-    feat_half = depth // 2
     share = u_ref.shape[1]
     block_width = 2 * share
     tasks = layers * CHUNKS
-    quarter = v_full.shape[2] // 4
+    quarter = w_full.shape[1] // 4
 
     dp, mp = lax.axis_index("dp"), lax.axis_index("mp")
     y_hi, z, core = dp // 8, lax.rem(dp // 2, 4), lax.rem(dp, 2)
@@ -56,28 +55,25 @@
     other = (1 - y_hi) * 4
 
     def piece(matrix, block):
-        layer = matrix // 2
-        if matrix % 2 == 0:
-            return v_full.at[
-                layer,
-                pl.ds(pl.multiple_of(core * feat_half, feat_half), feat_half),
-                pl.ds(pl.multiple_of(block * block_width, block_width), block_width),
-            ]
-        return u_full.at[layer, pl.ds(pl.multiple_of(block * block_width + core * share, share), share), :]
-
-    def move(matrix, block, number, device):
-        ref = piece(matrix, block)
-        return send(ref, ref, wss.at[matrix, number], wrs.at[matrix, number], device)
-
-    def swap_v(layer):
-        return send(v_ref.at[layer], vbuf.at[layer], w0s.at[layer], w0r.at[layer], partner)
-
-    def swap_u(layer):
-        place = u_full.at[layer, pl.ds(pl.multiple_of(own * block_width + core * share, share), share), :]
-        return send(u_ref.at[layer], place, w0s.at[layers + layer], w0r.at[layers + layer], partner)
+        first = pl.multiple_of(block * block_width + core * share, share)
+        return w_full.at[matrix, pl.ds(first, share), :]
+
+    def mine(matrix):
+        return (v_ref if matrix % 2 == 0 else u_ref).at[matrix // 2]
+
+    def move(matrix, block, number, device, source=None):
+        place = piece(matrix, block)
+        source = place if source is None else source
+        return send(source, place, wss.at[matrix, number], wrs.at[matrix, number], device)
 
     def far(matrix):
-        return [move(matrix, own, 0, y_far), move(matrix, own, 1, z_right), move(matrix, own, 2, z_left)]
+        source = mine(matrix)
+        return [
+            move(matrix, own, 0, y_far, source),
+            move(matrix, own, 1, z_right, source),
+            move(matrix, own, 2, z_left, source),
+            move(matrix, own, 14, partner, source),
+        ]
 
     def near(matrix):
         block = other + z
@@ -105,17 +101,9 @@
             copy.start()
 
     def weights_0(matrix):
-        layer = matrix // 2
-        if matrix % 2 == 0:
-            swap_v(layer).wait_recv()
-            mine, theirs = v_ref[layer], vbuf[layer]
-            first = core == 0
-            low = jnp.where(first, mine, theirs)
-            high = jnp.where(first, theirs, mine)
-            v_full[layer, :, pl.ds(pl.multiple_of(own * block_width, block_width), block_width)] = (
-                jnp.concatenate([low, high], axis=1)
-            )
         start(far(matrix))
+        first = pl.multiple_of(own * block_width + core * share, share)
+        w_full[matrix, pl.ds(first, share), :] = mine(matrix)[...]
 
     def weights_1(matrix):
         arrived(matrix, (0,))
@@ -130,11 +118,13 @@
         start(last(matrix))
 
     def weights_4(matrix):
-        arrived(matrix, (7, 8, 9, 10, 11, 12, 13))
-        if matrix % 2 == 1:
-            swap_u(matrix // 2).wait_recv()
+        arrived(matrix, (7, 8, 9, 10, 11, 12, 13, 14))
 
     weight_stages = (weights_0, weights_1, weights_2, weights_3, weights_4)
+
+    def weights(stage, matrix):
+        with jax.named_scope(f"w{stage}_{matrix}"):
+            weight_stages[stage](matrix)
 
     upper, lower = pl.ds(0, half), pl.ds(half, half)
 
@@ -170,8 +160,11 @@
     def stage_0(t):
         layer, chunk = t // CHUNKS, lax.rem(t, CHUNKS)
         for q in range(4):
-            part[t, q] = jnp.dot(
-                carried[chunk], v_full[layer, :, q * quarter : (q + 1) * quarter], preferred_element_type=F32
+            part[t, q] = lax.dot_general(
+                carried[chunk],
+                w_full[2 * layer, q * quarter : (q + 1) * quarter, :],
+                (((1,), (1,)), ((), ())),
+                preferred_element_type=F32,
             ).astype(BF16)
         start(first_hop(t))
 
@@ -214,11 +207,11 @@
         where = pl.ds(pl.multiple_of(chunk * rows, rows), rows)
         for j in range(4):
             columns = slice(j * depth // 4, (j + 1) * depth // 4)
-            total = b_ref[layer][:, columns]
+            total = b_ref[pl.ds(layer, 1), columns]
             for q in range(4):
                 total = total + jnp.dot(
                     rank[t, q],
-                    u_full[layer, q * quarter : (q + 1) * quarter, columns],
+                    w_full[2 * layer + 1, q * quarter : (q + 1) * quarter, columns],
                     preferred_element_type=F32,
                 )
             carried[chunk, :, columns] = (
@@ -229,24 +222,18 @@
         def _():
             out_ref[where, :] = carried[chunk]
 
-    for layer in range(layers):
-        swap_v(layer).start()
-    for layer in range(layers):
-        swap_u(layer).start()
-    for layer in range(layers):
-        u_full[layer, pl.ds(pl.multiple_of(own * block_width + core * share, share), share), :] = u_ref[layer]
-    weights_0(0)
+    weights(0, 0)
 
     @pl.loop(0, CHUNKS)
     def _(chunk):
         carried[chunk] = f_ref[pl.ds(pl.multiple_of(chunk * rows, rows), rows), :]
 
-    weights_1(0)
-    weights_2(0)
-    weights_3(0)
-    weights_0(1)
-    weights_1(1)
-    weights_4(0)
+    weights(1, 0)
+    weights(2, 0)
+    weights(3, 0)
+    weights(0, 1)
+    weights(1, 1)
+    weights(4, 0)
 
     plan = {}
     for stage in range(2, 5):
@@ -261,14 +248,15 @@
             @pl.when(i == when)
             def _(steps=steps):
                 for stage, matrix in steps:
-                    weight_stages[stage](matrix)
+                    weights(stage, matrix)
 
         for number, stage in ((4, stage_4), (3, stage_3), (2, stage_2), (1, stage_1), (5, stage_5), (0, stage_0)):
             t = i - LAG[number]
 
             @pl.when(jnp.logical_and(t >= 0, t < tasks))
-            def _(stage=stage, t=t):
-                stage(t)
+            def _(number=number, stage=stage, t=t):
+                with jax.named_scope(f"s{number}"):
+                    stage(t)
 
     @pl.loop(0, tasks)
     def _(t):
@@ -276,9 +264,6 @@
             for copy in copies(t):
                 copy.wait_send()
 
-    for layer in range(layers):
-        swap_v(layer).wait_send()
-        swap_u(layer).wait_send()
     for matrix in range(2 * layers):
         for copies in (far, near, onward, last):
             for copy in copies(matrix):
@@ -300,9 +285,7 @@
         in_specs=[vmem] * 4,
         out_specs=vmem,
         scratch_shapes=[
-            pltpu.VMEM((layers, depth, share), BF16),
-            pltpu.VMEM((layers, depth, rank), BF16),
-            pltpu.VMEM((layers, rank, depth), BF16),
+            pltpu.VMEM((2 * layers, rank, depth), BF16),
             pltpu.VMEM((CHUNKS, rows, depth), BF16),
             pltpu.VMEM((tasks, 4, rows, quarter), BF16),
             pltpu.VMEM((tasks, 4, rows, quarter), BF16),
@@ -313,15 +296,13 @@
             pltpu.VMEM((tasks, rows, quarter), BF16),
             dma((tasks, 11)),
             dma((tasks, 11)),
-            dma((2 * layers, 14)),
-            dma((2 * layers, 14)),
-            dma((2 * layers,)),
-            dma((2 * layers,)),
+            dma((2 * layers, 15)),
+            dma((2 * layers, 15)),
         ],
         compiler_params=pltpu.CompilerParams(
             collective_id=0, has_side_effects=True, vmem_limit_bytes=67043328
         ),
-    )(features, v_weight, u_weight, cross_bias.reshape(layers, 1, depth))
+    )(features, jnp.swapaxes(v_weight, 1, 2), u_weight, cross_bias)
 
 
 def solution(mesh):

time: 183 us -> 178 us (0.973)
  local copies, waits for them, and re-layouts: 6.55 us -> 3.08 us
    unnamed x2 -> x1, local copies, waits for them, and re-layouts: 5.23 us -> 3.08 us
where the time goes in v2:
time: 178 us
  Pallas kernels  175 us (98%)
  local copies, waits for them, and re-layouts  3.08 us (2%)
    pallas_call x1, Pallas kernels, local(): pl.pallas_call(kernel, out_shape=jax.ShapeDtypeStruct(features.shape, BF1...  175 us

profile of v2, /device:TPU:0, one launch (start us, length us, event | category | flops | bytes accessed | tf_op | source)
XLA Modules:
  0.0 178.2 jit_solution(1911455288476711228)
XLA Ops:
  0.0 175.1 %shard_map.46 = bf16[1024,1024]{1,0:T(8,128)(2,1)} custom-call(bf16[1024,1024]{1,0:T(8,128)(2,1)} %f_ref.1, bf16[3,64,1024]{2,1,0:T(8,128)(2,1)} %bitcast.1, bf16[3,64,1024]{2,1,0:T(8,128)(2,1)} %u_ref.1, f32[3,1024]{1,0:T(4,128)} %b_ref.1), custom_call_target="tpu_custom_call" | custom-call | tf_op jit(solution)/shard_map/pallas_call | solution.py:282
  175.1 3.1 %copy.6 = bf16[1024,1024]{1,0:T(8,128)(2,1)} copy(bf16[1024,1024]{1,0:T(8,128)(2,1)} %shard_map.46) | data formatting | bytes 4194304

commit v3 on v2

v3 whole, which is shorter than its diff:
```python
import jax
import jax.numpy as jnp
from jax import lax
from jax.experimental import pallas as pl
from jax.experimental.pallas import tpu as pltpu
from jax.sharding import PartitionSpec as P

MESH = pl.DeviceIdType.MESH
BF16 = jnp.bfloat16
F32 = jnp.float32

CHUNKS = 8
LAG = (0, 1, 2, 3, 4, 5)
ORDER = (4, 3, 2, 1, 5, 0)


def kernel(
    f_hbm, v_hbm, u_hbm, b_ref, out_hbm,
    features, w_full, carried, part, rank, rs1, s2, rs2, ysend, yrecv,
    ss, rs, wss, wrs, in_sem, own_sem, out_sem,
):
    layers = v_hbm.shape[0]
    matrices = 2 * layers
    rows = f_hbm.shape[0] // CHUNKS
    half = rows // 2
    depth = f_hbm.shape[1]
    share = u_hbm.shape[1]
    block_width = 2 * share
    tasks = layers * CHUNKS
    quarter = w_full.shape[1] // 4

    dp, mp = lax.axis_index("dp"), lax.axis_index("mp")
    y_hi, z, core = dp // 8, lax.rem(dp // 2, 4), lax.rem(dp, 2)
    y_lo, x = mp // 4, lax.rem(mp, 4)
    xr, xl, xo = lax.rem(x + 1, 4), lax.rem(x + 3, 4), lax.rem(x + 2, 4)
    zr, zl, zo = lax.rem(z + 1, 4), lax.rem(z + 3, 4), lax.rem(z + 2, 4)

    def at(y_hi=y_hi, z=z, core=core, y_lo=y_lo, x=x):
        return ((y_hi * 4 + z) * 2 + core, y_lo * 4 + x)

    right, left, across = at(x=xr), at(x=xl), at(y_lo=1 - y_lo)
    z_right, z_left, y_far, partner = at(z=zr), at(z=zl), at(y_hi=1 - y_hi), at(core=1 - core)

    barrier = pltpu.get_barrier_semaphore()
    for device in (right, left, across, z_right, z_left, y_far, partner):
        pl.semaphore_signal(barrier, inc=1, device_id=device, device_id_type=MESH)

    def send(src, dst, send_sem, recv_sem, device):
        return pltpu.make_async_remote_copy(
            src_ref=src, dst_ref=dst, send_sem=send_sem, recv_sem=recv_sem,
            device_id=device, device_id_type=MESH,
        )

    def start(copies):
        for copy in copies:
            copy.start()

    own, same, other = y_hi * 4 + z, y_hi * 4, (1 - y_hi) * 4

    def piece(matrix, block):
        first = pl.multiple_of(block * block_width + core * share, share)
        return w_full.at[matrix, pl.ds(first, share), :]

    def move(matrix, block, number, device):
        place = piece(matrix, block)
        return send(place, place, wss, wrs.at[matrix, number], device)

    def arrived(matrix, number, pieces):
        place = w_full.at[matrix, pl.ds(0, pieces * share), :]
        send(place, place, wss, wrs.at[matrix, number], partner).wait_recv()

    def own_piece(matrix):
        source = v_hbm if matrix % 2 == 0 else u_hbm
        return pltpu.make_async_copy(source.at[matrix // 2], piece(matrix, own), own_sem.at[matrix])

    def weights_0(matrix):
        start([move(matrix, own, 0, y_far), move(matrix, own, 1, z_right), move(matrix, own, 1, z_left),
               move(matrix, own, 4, partner)])

    def weights_1(matrix):
        arrived(matrix, 1, 2)
        start([move(matrix, same + zl, 3, z_right), move(matrix, same + zl, 4, partner),
               move(matrix, same + zr, 4, partner)])
        arrived(matrix, 0, 1)
        start([move(matrix, other + z, 2, z_right), move(matrix, other + z, 2, z_left),
               move(matrix, other + z, 4, partner)])

    def weights_2(matrix):
        arrived(matrix, 2, 2)
        start([move(matrix, other + zr, 3, z_left), move(matrix, other + zl, 4, partner),
               move(matrix, other + zr, 4, partner)])

    def weights_3(matrix):
        arrived(matrix, 3, 2)
        start([move(matrix, same + zo, 4, partner), move(matrix, other + zo, 4, partner)])

    def weights_4(matrix):
        arrived(matrix, 4, 8)

    weight_stages = (weights_0, weights_1, weights_2, weights_3, weights_4)
    weight_sends = 4 + 6 + 3 + 2

    upper, lower = pl.ds(0, half), pl.ds(half, half)

    def first_hop(t):
        start([
            send(part.at[t, xo, upper], rs1.at[t, 0], ss.at[0], rs.at[t, 0], right),
            send(part.at[t, xo, lower], rs1.at[t, 2], ss.at[0], rs.at[t, 0], left),
            send(part.at[t, xr, lower], rs1.at[t, 1], ss.at[0], rs.at[t, 1], right),
            send(part.at[t, xl, upper], rs1.at[t, 3], ss.at[0], rs.at[t, 1], left),
        ])

    def second_hop(t):
        start([
            send(s2.at[t, 0], rs2.at[t, 0], ss.at[1], rs.at[t, 1], right),
            send(s2.at[t, 1], rs2.at[t, 1], ss.at[1], rs.at[t, 1], left),
        ])

    def exchange(t):
        start([send(ysend.at[t], yrecv.at[t], ss.at[2], rs.at[t, 2], across)])

    def share_1(t):
        start([
            send(rank.at[t, x], rank.at[t, x], ss.at[3], rs.at[t, 3], right),
            send(rank.at[t, x], rank.at[t, x], ss.at[3], rs.at[t, 3], left),
        ])

    def share_2(t):
        start([
            send(rank.at[t, xl, upper], rank.at[t, xl, upper], ss.at[4], rs.at[t, 4], right),
            send(rank.at[t, xr, lower], rank.at[t, xr, lower], ss.at[4], rs.at[t, 4], left),
        ])

    def await_recv(t, number, size):
        send(size.at[t], size.at[t], ss.at[0], rs.at[t, number], right).wait_recv()

    def chunk_rows(chunk):
        return pl.ds(pl.multiple_of(chunk * rows, rows), rows)

    def result(chunk):
        return pltpu.make_async_copy(carried.at[chunk], out_hbm.at[chunk_rows(chunk), :], out_sem.at[0])

    def stage_0(t):
        layer, chunk = t // CHUNKS, lax.rem(t, CHUNKS)
        for q in range(4):
            part[t, q] = lax.dot_general(
                carried[chunk],
                w_full[2 * layer, q * quarter : (q + 1) * quarter, :],
                (((1,), (1,)), ((), ())),
                preferred_element_type=F32,
            ).astype(BF16)
        first_hop(t)

    def stage_1(t):
        await_recv(t, 0, rs2)
        s2[t, 0] = (part[t, xr, upper].astype(F32) + rs1[t, 0].astype(F32)).astype(BF16)
        s2[t, 1] = (part[t, xl, lower].astype(F32) + rs1[t, 2].astype(F32)).astype(BF16)
        second_hop(t)

    def stage_2(t):
        await_recv(t, 1, rs1)
        ysend[t, upper] = (
            part[t, x, upper].astype(F32) + rs2[t, 0].astype(F32) + rs1[t, 3].astype(F32)
        ).astype(BF16)
        ysend[t, lower] = (
            part[t, x, lower].astype(F32) + rs2[t, 1].astype(F32) + rs1[t, 1].astype(F32)
        ).astype(BF16)
        exchange(t)

    def stage_3(t):
        await_recv(t, 2, yrecv)
        rank[t, x] = (ysend[t].astype(F32) + yrecv[t].astype(F32)).astype(BF16)
        share_1(t)

    def stage_4(t):
        await_recv(t, 3, rs1)
        share_2(t)

    def stage_5(t):
        layer, chunk = t // CHUNKS, lax.rem(t, CHUNKS)
        await_recv(t, 4, rs2)
        for j in range(4):
            columns = slice(j * depth // 4, (j + 1) * depth // 4)
            total = b_ref[pl.ds(layer, 1), columns]
            for q in range(4):
                total = total + jnp.dot(
                    rank[t, q],
                    w_full[2 * layer + 1, q * quarter : (q + 1) * quarter, columns],
                    preferred_element_type=F32,
                )
            carried[chunk, :, columns] = (
                features[chunk_rows(chunk), columns].astype(F32) * total + carried[chunk, :, columns].astype(F32)
            ).astype(BF16)

        @pl.when(layer == layers - 1)
        def _():
            result(chunk).start()

    stages = (stage_0, stage_1, stage_2, stage_3, stage_4, stage_5)

    for matrix in range(matrices):
        own_piece(matrix).start()
    fetches = [pltpu.make_async_copy(f_hbm, features, in_sem.at[0])] + [
        pltpu.make_async_copy(f_hbm.at[pl.ds(chunk * rows, rows), :], carried.at[chunk], in_sem.at[1])
        for chunk in range(CHUNKS)
    ]
    start(fetches)
    with jax.named_scope("barrier"):
        pl.semaphore_wait(barrier, 7)
    with jax.named_scope("fetch"):
        for matrix in range(matrices):
            own_piece(matrix).wait()
    with jax.named_scope("v0"):
        weights_0(0)
        weights_1(0)
        weights_2(0)
    weights_0(1)
    with jax.named_scope("v0b"):
        weights_3(0)
    with jax.named_scope("u0"):
        weights_1(1)
    with jax.named_scope("v0c"):
        weights_4(0)
        for fetch in fetches:
            fetch.wait()

    @pl.loop(0, tasks + LAG[5])
    def _(i):
        for number in ORDER:
            t = i - LAG[number]

            @pl.when(jnp.logical_and(t >= 0, t < tasks))
            def _(number=number, t=t):
                with jax.named_scope(f"s{number}"):
                    stages[number](t)

        for number in range(5):
            turn = i + 6 - number
            matrix = turn // 4

            @pl.when(jnp.logical_and(lax.rem(turn, 4) == 0, jnp.logical_and(matrix >= 1, matrix < matrices)))
            def _(number=number, matrix=matrix):
                with jax.named_scope(f"w{number}"):
                    weight_stages[number](matrix)

    with jax.named_scope("end"):
        for number, size in ((0, rs1), (1, rs2), (2, yrecv), (3, rs1), (4, rs2)):
            send(size, size, ss.at[number], rs.at[0, 0], right).wait_send()
        for matrix in range(matrices):
            place = w_full.at[matrix, pl.ds(0, weight_sends * share), :]
            send(place, place, wss, wrs.at[0, 0], right).wait_send()
        for chunk in range(CHUNKS):
            result(chunk).wait()


def local(features, v_weight, u_weight, cross_bias):
    layers, depth, share = v_weight.shape
    rank = share * lax.axis_size("dp")
    rows = features.shape[0] // CHUNKS
    half = rows // 2
    quarter = rank // 4
    tasks = layers * CHUNKS
    dma = pltpu.SemaphoreType.DMA
    anywhere = pl.BlockSpec(memory_space=pl.ANY)
    return pl.pallas_call(
        kernel,
        out_shape=jax.ShapeDtypeStruct(features.shape, BF16),
        in_specs=[anywhere] * 3 + [pl.BlockSpec(memory_space=pltpu.VMEM)],
        out_specs=anywhere,
        scratch_shapes=[
            pltpu.VMEM(features.shape, BF16),
            pltpu.VMEM((2 * layers, rank, depth), BF16),
            pltpu.VMEM((CHUNKS, rows, depth), BF16),
            pltpu.VMEM((tasks, 4, rows, quarter), BF16),
            pltpu.VMEM((tasks, 4, rows, quarter), BF16),
            pltpu.VMEM((tasks, 4, half, quarter), BF16),
            pltpu.VMEM((tasks, 2, half, quarter), BF16),
            pltpu.VMEM((tasks, 2, half, quarter), BF16),
            pltpu.VMEM((tasks, rows, quarter), BF16),
            pltpu.VMEM((tasks, rows, quarter), BF16),
            dma((5,)),
            dma((tasks, 5)),
            dma,
            dma((2 * layers, 5)),
            dma((2,)),
            dma((2 * layers,)),
            dma((1,)),
        ],
        compiler_params=pltpu.CompilerParams(
            collective_id=0, has_side_effects=True, vmem_limit_bytes=67043328
        ),
    )(features, jnp.swapaxes(v_weight, 1, 2), u_weight, cross_bias)


def solution(mesh):
    return jax.shard_map(
        local,
        mesh=mesh,
        in_specs=(P("dp", "mp"), P(None, "mp", "dp"), P(None, "dp", "mp"), P(None, "mp")),
        out_specs=P("dp", "mp"),
        check_vma=False,
    )
```

time: 178 us -> 167 us (0.938)
  Pallas kernels: 175 us -> 164 us
    pallas_call x1, Pallas kernels: 175 us -> 164 us  [local(): pl.pallas_call(kernel, out_shape=jax.ShapeDtypeStruct(features.shape, BF1...]
where the time goes in v3:
time: 167 us
  Pallas kernels  164 us (98%)
  local copies, waits for them, and re-layouts  3.08 us (2%)
    pallas_call x1, Pallas kernels, local(): pl.pallas_call(kernel, out_shape=jax.ShapeDtypeStruct(features.shape, BF1...  164 us

profile of v3, /device:TPU:0, one launch (start us, length us, event | category | flops | bytes accessed | tf_op | source)
XLA Modules:
  0.0 167.1 jit_solution(8027911172081229154)
XLA Ops:
  0.0 164.0 %shard_map.46 = bf16[1024,1024]{1,0:T(8,128)(2,1)} custom-call(bf16[1024,1024]{1,0:T(8,128)(2,1)} %f_hbm.1, bf16[3,64,1024]{2,1,0:T(8,128)(2,1)} %bitcast.1, bf16[3,64,1024]{2,1,0:T(8,128)(2,1)} %u_hbm.1, f32[3,1024]{1,0:T(4,128)} %b_ref.1), custom_call_target="tpu_custom_call" | custom-call | tf_op jit(solution)/shard_map/pallas_call | solution.py:265
  164.0 3.1 %copy.6 = bf16[1024,1024]{1,0:T(8,128)(2,1)} copy(bf16[1024,1024]{1,0:T(8,128)(2,1)} %shard_map.46) | data formatting | bytes 4194304

commit v4 on v3

--- a/solution.py
+++ b/solution.py
@@ -10,19 +10,23 @@
 F32 = jnp.float32
 
 CHUNKS = 8
-LAG = (0, 1, 2, 3, 4, 5)
-ORDER = (4, 3, 2, 1, 5, 0)
+LAG = (0, 1, 2, 3, 4, 5, 6)
+WLAG = (0, 3, 5, 7, 8)
+EARLY = 32
+UPPER_A, UPPER_B = 16, 48
 
 
 def kernel(
     f_hbm, v_hbm, u_hbm, b_ref, out_hbm,
-    features, w_full, carried, part, rank, rs1, s2, rs2, ysend, yrecv,
+    features, w_full, carried,
+    part_b, far_b, mid_b, near_b, sum_b, across_b, rank_b,
+    part_a, across_a, sum_a, far_a, mid_a, near_a, rank_a,
     ss, rs, wss, wrs, in_sem, own_sem, out_sem,
 ):
     layers = v_hbm.shape[0]
     matrices = 2 * layers
     rows = f_hbm.shape[0] // CHUNKS
-    half = rows // 2
+    late = rows - EARLY
     depth = f_hbm.shape[1]
     share = u_hbm.shape[1]
     block_width = 2 * share
@@ -100,36 +104,58 @@
     weight_stages = (weights_0, weights_1, weights_2, weights_3, weights_4)
     weight_sends = 4 + 6 + 3 + 2
 
-    upper, lower = pl.ds(0, half), pl.ds(half, half)
-
-    def first_hop(t):
-        start([
-            send(part.at[t, xo, upper], rs1.at[t, 0], ss.at[0], rs.at[t, 0], right),
-            send(part.at[t, xo, lower], rs1.at[t, 2], ss.at[0], rs.at[t, 0], left),
-            send(part.at[t, xr, lower], rs1.at[t, 1], ss.at[0], rs.at[t, 1], right),
-            send(part.at[t, xl, upper], rs1.at[t, 3], ss.at[0], rs.at[t, 1], left),
-        ])
-
-    def second_hop(t):
-        start([
-            send(s2.at[t, 0], rs2.at[t, 0], ss.at[1], rs.at[t, 1], right),
-            send(s2.at[t, 1], rs2.at[t, 1], ss.at[1], rs.at[t, 1], left),
-        ])
-
-    def exchange(t):
-        start([send(ysend.at[t], yrecv.at[t], ss.at[2], rs.at[t, 2], across)])
-
-    def share_1(t):
-        start([
-            send(rank.at[t, x], rank.at[t, x], ss.at[3], rs.at[t, 3], right),
-            send(rank.at[t, x], rank.at[t, x], ss.at[3], rs.at[t, 3], left),
-        ])
-
-    def share_2(t):
-        start([
-            send(rank.at[t, xl, upper], rank.at[t, xl, upper], ss.at[4], rs.at[t, 4], right),
-            send(rank.at[t, xr, lower], rank.at[t, xr, lower], ss.at[4], rs.at[t, 4], left),
-        ])
+    def to_right_and_left(t, rows, upper, part, far, mid, near, rank, first):
+        upper, lower = pl.ds(0, upper), pl.ds(upper, rows - upper)
+
+        def hop_1():
+            start([
+                send(part(xo).at[upper], far.at[t, upper], ss.at[first], rs.at[t, first], right),
+                send(part(xo).at[lower], far.at[t, lower], ss.at[first], rs.at[t, first], left),
+                send(part(xr).at[lower], near.at[t, 0, lower], ss.at[first], rs.at[t, first + 1], right),
+                send(part(xl).at[upper], near.at[t, 0, upper], ss.at[first], rs.at[t, first + 1], left),
+            ])
+
+        def hop_2():
+            await_recv(t, first, far)
+            mid[t, upper] = (part(xr)[upper].astype(F32) + far[t, upper].astype(F32)).astype(BF16)
+            mid[t, lower] = (part(xl)[lower].astype(F32) + far[t, lower].astype(F32)).astype(BF16)
+            start([
+                send(mid.at[t, upper], near.at[t, 1, upper], ss.at[first + 1], rs.at[t, first + 1], right),
+                send(mid.at[t, lower], near.at[t, 1, lower], ss.at[first + 1], rs.at[t, first + 1], left),
+            ])
+
+        def total():
+            await_recv(t, first + 1, near)
+            return (
+                part(x)[...].astype(F32) + near[t, 0].astype(F32) + near[t, 1].astype(F32)
+            ).astype(BF16)
+
+        def share_1():
+            start([
+                send(rank(x), rank(x), ss.at[first + 2], rs.at[t, first + 2], right),
+                send(rank(x), rank(x), ss.at[first + 2], rs.at[t, first + 2], left),
+            ])
+
+        def share_2():
+            await_recv(t, first + 2, near)
+            start([
+                send(rank(xl).at[lower], rank(xl).at[lower], ss.at[first + 3], rs.at[t, first + 3], right),
+                send(rank(xr).at[upper], rank(xr).at[upper], ss.at[first + 3], rs.at[t, first + 3], left),
+            ])
+
+        return hop_1, hop_2, total, share_1, share_2
+
+    def ways(t):
+        late_ways = to_right_and_left(
+            t, late, UPPER_B, lambda q: part_b.at[t, q], far_b, mid_b, near_b, lambda q: rank_b.at[t, q], 0
+        )
+        early_ways = to_right_and_left(
+            t, EARLY, UPPER_A, lambda q: sum_a.at[t, q], far_a, mid_a, near_a, lambda q: rank_a.at[t, y_lo, q], 4
+        )
+        return late_ways, early_ways
+
+    def over_y(t, src, dst, number):
+        send(src, dst, ss.at[number], rs.at[t, number], across).start()
 
     def await_recv(t, number, size):
         send(size.at[t], size.at[t], ss.at[0], rs.at[t, number], right).wait_recv()
@@ -143,48 +169,64 @@
     def stage_0(t):
         layer, chunk = t // CHUNKS, lax.rem(t, CHUNKS)
         for q in range(4):
-            part[t, q] = lax.dot_general(
+            piece_q = lax.dot_general(
                 carried[chunk],
                 w_full[2 * layer, q * quarter : (q + 1) * quarter, :],
                 (((1,), (1,)), ((), ())),
                 preferred_element_type=F32,
             ).astype(BF16)
-        first_hop(t)
+            part_b[t, q] = piece_q[:late]
+            part_a[t, 0, q] = piece_q[late:, : quarter // 2]
+            part_a[t, 1, q] = piece_q[late:, quarter // 2 :]
+        over_y(t, part_a.at[t, 1 - y_lo], across_a.at[t], 9)
+        ways(t)[0][0]()
 
     def stage_1(t):
-        await_recv(t, 0, rs2)
-        s2[t, 0] = (part[t, xr, upper].astype(F32) + rs1[t, 0].astype(F32)).astype(BF16)
-        s2[t, 1] = (part[t, xl, lower].astype(F32) + rs1[t, 2].astype(F32)).astype(BF16)
-        second_hop(t)
+        late_ways, early_ways = ways(t)
+        await_recv(t, 9, across_a)
+        sum_a[t] = (part_a[t, y_lo].astype(F32) + across_a[t].astype(F32)).astype(BF16)
+        early_ways[0]()
+        late_ways[1]()
 
     def stage_2(t):
-        await_recv(t, 1, rs1)
-        ysend[t, upper] = (
-            part[t, x, upper].astype(F32) + rs2[t, 0].astype(F32) + rs1[t, 3].astype(F32)
-        ).astype(BF16)
-        ysend[t, lower] = (
-            part[t, x, lower].astype(F32) + rs2[t, 1].astype(F32) + rs1[t, 1].astype(F32)
-        ).astype(BF16)
-        exchange(t)
+        late_ways, early_ways = ways(t)
+        early_ways[1]()
+        sum_b[t] = late_ways[2]()
+        over_y(t, sum_b.at[t], across_b.at[t], 8)
 
     def stage_3(t):
-        await_recv(t, 2, yrecv)
-        rank[t, x] = (ysend[t].astype(F32) + yrecv[t].astype(F32)).astype(BF16)
-        share_1(t)
+        late_ways, early_ways = ways(t)
+        rank_a[t, y_lo, x] = early_ways[2]()
+        early_ways[3]()
+        await_recv(t, 8, across_b)
+        rank_b[t, x] = (sum_b[t].astype(F32) + across_b[t].astype(F32)).astype(BF16)
+        late_ways[3]()
 
     def stage_4(t):
-        await_recv(t, 3, rs1)
-        share_2(t)
+        late_ways, early_ways = ways(t)
+        early_ways[4]()
+        late_ways[4]()
 
     def stage_5(t):
+        await_recv(t, 7, far_a)
+        over_y(t, rank_a.at[t, y_lo], rank_a.at[t, y_lo], 10)
+
+    def stage_6(t):
         layer, chunk = t // CHUNKS, lax.rem(t, CHUNKS)
-        await_recv(t, 4, rs2)
+        await_recv(t, 3, far_b)
+        await_recv(t, 10, across_a)
+        lhs = [
+            jnp.concatenate(
+                [rank_b[t, q], jnp.concatenate([rank_a[t, 0, q], rank_a[t, 1, q]], axis=1)], axis=0
+            )
+            for q in range(4)
+        ]
         for j in range(4):
             columns = slice(j * depth // 4, (j + 1) * depth // 4)
             total = b_ref[pl.ds(layer, 1), columns]
             for q in range(4):
                 total = total + jnp.dot(
-                    rank[t, q],
+                    lhs[q],
                     w_full[2 * layer + 1, q * quarter : (q + 1) * quarter, columns],
                     preferred_element_type=F32,
                 )
@@ -196,7 +238,7 @@
         def _():
             result(chunk).start()
 
-    stages = (stage_0, stage_1, stage_2, stage_3, stage_4, stage_5)
+    stages = (stage_0, stage_1, stage_2, stage_3, stage_4, stage_5, stage_6)
 
     for matrix in range(matrices):
         own_piece(matrix).start()
@@ -217,16 +259,26 @@
     weights_0(1)
     with jax.named_scope("v0b"):
         weights_3(0)
-    with jax.named_scope("u0"):
-        weights_1(1)
     with jax.named_scope("v0c"):
         weights_4(0)
         for fetch in fetches:
             fetch.wait()
 
-    @pl.loop(0, tasks + LAG[5])
+    def weights_at(i, number):
+        turn = i - WLAG[number]
+        first = turn == -WLAG[1]
+        matrix = jnp.where(first, 1, turn // 4 + 2)
+        regular = jnp.logical_and(jnp.logical_and(turn >= 0, lax.rem(turn, 4) == 0), matrix < matrices)
+
+        @pl.when(jnp.logical_or(first, regular))
+        def _():
+            with jax.named_scope(f"w{number}"):
+                weight_stages[number](matrix)
+
+    @pl.loop(0, tasks + LAG[6])
     def _(i):
-        for number in ORDER:
+        weights_at(i, 4)
+        for number in range(7):
             t = i - LAG[number]
 
             @pl.when(jnp.logical_and(t >= 0, t < tasks))
@@ -234,17 +286,14 @@
                 with jax.named_scope(f"s{number}"):
                     stages[number](t)
 
-        for number in range(5):
-            turn = i + 6 - number
-            matrix = turn // 4
-
-            @pl.when(jnp.logical_and(lax.rem(turn, 4) == 0, jnp.logical_and(matrix >= 1, matrix < matrices)))
-            def _(number=number, matrix=matrix):
-                with jax.named_scope(f"w{number}"):
-                    weight_stages[number](matrix)
+        for number in range(4):
+            weights_at(i, number)
 
     with jax.named_scope("end"):
-        for number, size in ((0, rs1), (1, rs2), (2, yrecv), (3, rs1), (4, rs2)):
+        sent = (
+            near_b, far_b, near_b, far_b, near_a, far_a, near_a, far_a, across_b, across_a, across_a
+        )
+        for number, size in enumerate(sent):
             send(size, size, ss.at[number], rs.at[0, 0], right).wait_send()
         for matrix in range(matrices):
             place = w_full.at[matrix, pl.ds(0, weight_sends * share), :]
@@ -257,7 +306,7 @@
     layers, depth, share = v_weight.shape
     rank = share * lax.axis_size("dp")
     rows = features.shape[0] // CHUNKS
-    half = rows // 2
+    late = rows - EARLY
     quarter = rank // 4
     tasks = layers * CHUNKS
     dma = pltpu.SemaphoreType.DMA
@@ -271,15 +320,22 @@
             pltpu.VMEM(features.shape, BF16),
             pltpu.VMEM((2 * layers, rank, depth), BF16),
             pltpu.VMEM((CHUNKS, rows, depth), BF16),
-            pltpu.VMEM((tasks, 4, rows, quarter), BF16),
-            pltpu.VMEM((tasks, 4, rows, quarter), BF16),
-            pltpu.VMEM((tasks, 4, half, quarter), BF16),
-            pltpu.VMEM((tasks, 2, half, quarter), BF16),
-            pltpu.VMEM((tasks, 2, half, quarter), BF16),
-            pltpu.VMEM((tasks, rows, quarter), BF16),
-            pltpu.VMEM((tasks, rows, quarter), BF16),
-            dma((5,)),
-            dma((tasks, 5)),
+            pltpu.VMEM((tasks, 4, late, quarter), BF16),
+            pltpu.VMEM((tasks, late, quarter), BF16),
+            pltpu.VMEM((tasks, late, quarter), BF16),
+            pltpu.VMEM((tasks, 2, late, quarter), BF16),
+            pltpu.VMEM((tasks, late, quarter), BF16),
+            pltpu.VMEM((tasks, late, quarter), BF16),
+            pltpu.VMEM((tasks, 4, late, quarter), BF16),
+            pltpu.VMEM((tasks, 2, 4, EARLY, quarter // 2), BF16),
+            pltpu.VMEM((tasks, 4, EARLY, quarter // 2), BF16),
+            pltpu.VMEM((tasks, 4, EARLY, quarter // 2), BF16),
+            pltpu.VMEM((tasks, EARLY, quarter // 2), BF16),
+            pltpu.VMEM((tasks, EARLY, quarter // 2), BF16),
+            pltpu.VMEM((tasks, 2, EARLY, quarter // 2), BF16),
+            pltpu.VMEM((tasks, 2, 4, EARLY, quarter // 2), BF16),
+            dma((11,)),
+            dma((tasks, 11)),
             dma,
             dma((2 * layers, 5)),
             dma((2,)),

time: 167 us -> 146 us (0.87)
  Pallas kernels: 164 us -> 142 us
    pallas_call x1, Pallas kernels: 164 us -> 142 us  [local(): pl.pallas_call(kernel, out_shape=jax.ShapeDtypeStruct(features.shape, BF1...]
where the time goes in v4:
time: 146 us; the launch traced here: 145 us
  Pallas kernels  142 us (97%)
  local copies, waits for them, and re-layouts  3.08 us (2%)
    pallas_call x1, Pallas kernels, local(): pl.pallas_call(kernel, out_shape=jax.ShapeDtypeStruct(features.shape, BF1...  142 us
    unnamed x1, local copies, waits for them, and re-layouts  3.08 us

profile of v4, /device:TPU:0, one launch (start us, length us, event | category | flops | bytes accessed | tf_op | source)
XLA Modules:
  0.0 145.3 jit_solution(4701412393705929912)
XLA Ops:
  0.0 142.3 %shard_map.46 = bf16[1024,1024]{1,0:T(8,128)(2,1)} custom-call(bf16[1024,1024]{1,0:T(8,128)(2,1)} %f_hbm.1, bf16[3,64,1024]{2,1,0:T(8,128)(2,1)} %bitcast.1, bf16[3,64,1024]{2,1,0:T(8,128)(2,1)} %u_hbm.1, f32[3,1024]{1,0:T(4,128)} %b_ref.1), custom_call_target="tpu_custom_call" | custom-call | tf_op jit(solution)/shard_map/pallas_call | solution.py:314
  142.3 3.1 %copy.6 = bf16[1024,1024]{1,0:T(8,128)(2,1)} copy(bf16[1024,1024]{1,0:T(8,128)(2,1)} %shard_map.46) | data formatting | bytes 4194304

commit v5 on v4

--- a/solution.py
+++ b/solution.py
@@ -10,18 +10,20 @@
 F32 = jnp.float32
 
 CHUNKS = 8
-LAG = (0, 1, 2, 3, 4, 5, 6)
-WLAG = (0, 3, 5, 7, 8)
-EARLY = 32
-UPPER_A, UPPER_B = 16, 48
+LAG = (0, 1, 2, 3, 4, 5, 7)
+WLAG = (0, 2, 4, 6, 8)
+EARLY = 48
+UPPER_A, UPPER_B = 32, 48
+SLOTS = 8
+PARTS = 4
 
 
 def kernel(
-    f_hbm, v_hbm, u_hbm, b_ref, out_hbm,
-    features, w_full, carried,
+    f_hbm, v_hbm, u_hbm, b_hbm, out_ref,
+    features, w_full, carried, bias,
     part_b, far_b, mid_b, near_b, sum_b, across_b, rank_b,
     part_a, across_a, sum_a, far_a, mid_a, near_a, rank_a,
-    ss, rs, wss, wrs, in_sem, own_sem, out_sem,
+    ss, rs, wss, wrs, v0s, in_sem, own_sem,
 ):
     layers = v_hbm.shape[0]
     matrices = 2 * layers
@@ -78,8 +80,7 @@
         return pltpu.make_async_copy(source.at[matrix // 2], piece(matrix, own), own_sem.at[matrix])
 
     def weights_0(matrix):
-        start([move(matrix, own, 0, y_far), move(matrix, own, 1, z_right), move(matrix, own, 1, z_left),
-               move(matrix, own, 4, partner)])
+        start([move(matrix, own, 1, z_right), move(matrix, own, 1, z_left), move(matrix, own, 4, partner)])
 
     def weights_1(matrix):
         arrived(matrix, 1, 2)
@@ -104,15 +105,52 @@
     weight_stages = (weights_0, weights_1, weights_2, weights_3, weights_4)
     weight_sends = 4 + 6 + 3 + 2
 
+    def down_0():
+        step = share // PARTS
+
+        def sub(block, s, sem, device):
+            first = pl.multiple_of(block * block_width + core * share + s * step, step)
+            place = w_full.at[0, pl.ds(first, step), :]
+            return send(place, place, wss, sem, device)
+
+        def landed(kind, s):
+            sub(own, s, v0s.at[kind, s], partner).wait_recv()
+
+        for s in range(PARTS):
+            start([sub(own, s, v0s.at[0, s], z_right), sub(own, s, wrs.at[0, 0], z_left), sub(own, s, v0s.at[1, s], y_far)])
+        move(0, own, 4, partner).start()
+        for matrix in range(1, matrices):
+            move(matrix, own, 0, y_far).start()
+        for s in range(PARTS):
+            landed(0, s)
+            sub(same + zl, s, wrs.at[0, 2], z_right).start()
+            landed(1, s)
+            start([sub(other + z, s, wrs.at[0, 1], z_right), sub(other + z, s, v0s.at[2, s], z_left)])
+        start([move(0, same + zl, 4, partner), move(0, other + z, 4, partner)])
+        arrived(0, 0, 1)
+        move(0, same + zr, 4, partner).start()
+        for s in range(PARTS):
+            landed(2, s)
+            sub(other + zr, s, wrs.at[0, 3], z_left).start()
+        move(0, other + zr, 4, partner).start()
+        arrived(0, 1, 1)
+        move(0, other + zl, 4, partner).start()
+        weights_0(1)
+        arrived(0, 2, 1)
+        move(0, same + zo, 4, partner).start()
+        arrived(0, 3, 1)
+        move(0, other + zo, 4, partner).start()
+        arrived(0, 4, 8)
+
     def to_right_and_left(t, rows, upper, part, far, mid, near, rank, first):
         upper, lower = pl.ds(0, upper), pl.ds(upper, rows - upper)
 
         def hop_1():
             start([
-                send(part(xo).at[upper], far.at[t, upper], ss.at[first], rs.at[t, first], right),
-                send(part(xo).at[lower], far.at[t, lower], ss.at[first], rs.at[t, first], left),
-                send(part(xr).at[lower], near.at[t, 0, lower], ss.at[first], rs.at[t, first + 1], right),
-                send(part(xl).at[upper], near.at[t, 0, upper], ss.at[first], rs.at[t, first + 1], left),
+                send(part(xo).at[upper], far.at[t, upper], ss.at[first], rs.at[lax.rem(t, SLOTS), first], right),
+                send(part(xo).at[lower], far.at[t, lower], ss.at[first], rs.at[lax.rem(t, SLOTS), first], left),
+                send(part(xr).at[lower], near.at[t, 0, lower], ss.at[first], rs.at[lax.rem(t, SLOTS), first + 1], right),
+                send(part(xl).at[upper], near.at[t, 0, upper], ss.at[first], rs.at[lax.rem(t, SLOTS), first + 1], left),
             ])
 
         def hop_2():
@@ -120,8 +158,8 @@
             mid[t, upper] = (part(xr)[upper].astype(F32) + far[t, upper].astype(F32)).astype(BF16)
             mid[t, lower] = (part(xl)[lower].astype(F32) + far[t, lower].astype(F32)).astype(BF16)
             start([
-                send(mid.at[t, upper], near.at[t, 1, upper], ss.at[first + 1], rs.at[t, first + 1], right),
-                send(mid.at[t, lower], near.at[t, 1, lower], ss.at[first + 1], rs.at[t, first + 1], left),
+                send(mid.at[t, upper], near.at[t, 1, upper], ss.at[first + 1], rs.at[lax.rem(t, SLOTS), first + 1], right),
+                send(mid.at[t, lower], near.at[t, 1, lower], ss.at[first + 1], rs.at[lax.rem(t, SLOTS), first + 1], left),
             ])
 
         def total():
@@ -132,15 +170,15 @@
 
         def share_1():
             start([
-                send(rank(x), rank(x), ss.at[first + 2], rs.at[t, first + 2], right),
-                send(rank(x), rank(x), ss.at[first + 2], rs.at[t, first + 2], left),
+                send(rank(x), rank(x), ss.at[first + 2], rs.at[lax.rem(t, SLOTS), first + 2], right),
+                send(rank(x), rank(x), ss.at[first + 2], rs.at[lax.rem(t, SLOTS), first + 2], left),
             ])
 
         def share_2():
             await_recv(t, first + 2, near)
             start([
-                send(rank(xl).at[lower], rank(xl).at[lower], ss.at[first + 3], rs.at[t, first + 3], right),
-                send(rank(xr).at[upper], rank(xr).at[upper], ss.at[first + 3], rs.at[t, first + 3], left),
+                send(rank(xl).at[lower], rank(xl).at[lower], ss.at[first + 3], rs.at[lax.rem(t, SLOTS), first + 3], right),
+                send(rank(xr).at[upper], rank(xr).at[upper], ss.at[first + 3], rs.at[lax.rem(t, SLOTS), first + 3], left),
             ])
 
         return hop_1, hop_2, total, share_1, share_2
@@ -155,16 +193,13 @@
         return late_ways, early_ways
 
     def over_y(t, src, dst, number):
-        send(src, dst, ss.at[number], rs.at[t, number], across).start()
+        send(src, dst, ss.at[number], rs.at[lax.rem(t, SLOTS), number], across).start()
 
     def await_recv(t, number, size):
-        send(size.at[t], size.at[t], ss.at[0], rs.at[t, number], right).wait_recv()
+        send(size.at[t], size.at[t], ss.at[0], rs.at[lax.rem(t, SLOTS), number], right).wait_recv()
 
     def chunk_rows(chunk):
         return pl.ds(pl.multiple_of(chunk * rows, rows), rows)
-
-    def result(chunk):
-        return pltpu.make_async_copy(carried.at[chunk], out_hbm.at[chunk_rows(chunk), :], out_sem.at[0])
 
     def stage_0(t):
         layer, chunk = t // CHUNKS, lax.rem(t, CHUNKS)
@@ -223,26 +258,27 @@
         ]
         for j in range(4):
             columns = slice(j * depth // 4, (j + 1) * depth // 4)
-            total = b_ref[pl.ds(layer, 1), columns]
+            total = bias[pl.ds(layer, 1), columns]
             for q in range(4):
                 total = total + jnp.dot(
                     lhs[q],
                     w_full[2 * layer + 1, q * quarter : (q + 1) * quarter, columns],
                     preferred_element_type=F32,
                 )
-            carried[chunk, :, columns] = (
+            new = (
                 features[chunk_rows(chunk), columns].astype(F32) * total + carried[chunk, :, columns].astype(F32)
             ).astype(BF16)
-
-        @pl.when(layer == layers - 1)
-        def _():
-            result(chunk).start()
+            carried[chunk, :, columns] = new
+
+            @pl.when(layer == layers - 1)
+            def _(columns=columns, new=new):
+                out_ref[chunk_rows(chunk), columns] = new
 
     stages = (stage_0, stage_1, stage_2, stage_3, stage_4, stage_5, stage_6)
 
     for matrix in range(matrices):
         own_piece(matrix).start()
-    fetches = [pltpu.make_async_copy(f_hbm, features, in_sem.at[0])] + [
+    fetches = [pltpu.make_async_copy(f_hbm, features, in_sem.at[0]), pltpu.make_async_copy(b_hbm, bias, in_sem.at[2])] + [
         pltpu.make_async_copy(f_hbm.at[pl.ds(chunk * rows, rows), :], carried.at[chunk], in_sem.at[1])
         for chunk in range(CHUNKS)
     ]
@@ -253,14 +289,8 @@
         for matrix in range(matrices):
             own_piece(matrix).wait()
     with jax.named_scope("v0"):
-        weights_0(0)
-        weights_1(0)
-        weights_2(0)
-    weights_0(1)
-    with jax.named_scope("v0b"):
-        weights_3(0)
+        down_0()
     with jax.named_scope("v0c"):
-        weights_4(0)
         for fetch in fetches:
             fetch.wait()
 
@@ -298,8 +328,6 @@
         for matrix in range(matrices):
             place = w_full.at[matrix, pl.ds(0, weight_sends * share), :]
             send(place, place, wss, wrs.at[0, 0], right).wait_send()
-        for chunk in range(CHUNKS):
-            result(chunk).wait()
 
 
 def local(features, v_weight, u_weight, cross_bias):
@@ -310,16 +338,21 @@
     quarter = rank // 4
     tasks = layers * CHUNKS
     dma = pltpu.SemaphoreType.DMA
-    anywhere = pl.BlockSpec(memory_space=pl.ANY)
+    anywhere = pl.BlockSpec(memory_space=pltpu.HBM)
+    arguments = [
+        pltpu.with_memory_space_constraint(array, pltpu.HBM)
+        for array in (features, jnp.swapaxes(v_weight, 1, 2), u_weight, cross_bias)
+    ]
     return pl.pallas_call(
         kernel,
         out_shape=jax.ShapeDtypeStruct(features.shape, BF16),
-        in_specs=[anywhere] * 3 + [pl.BlockSpec(memory_space=pltpu.VMEM)],
-        out_specs=anywhere,
+        in_specs=[anywhere] * 4,
+        out_specs=pl.BlockSpec(memory_space=pltpu.VMEM),
         scratch_shapes=[
             pltpu.VMEM(features.shape, BF16),
             pltpu.VMEM((2 * layers, rank, depth), BF16),
             pltpu.VMEM((CHUNKS, rows, depth), BF16),
+            pltpu.VMEM(cross_bias.shape, F32),
             pltpu.VMEM((tasks, 4, late, quarter), BF16),
             pltpu.VMEM((tasks, late, quarter), BF16),
             pltpu.VMEM((tasks, late, quarter), BF16),
@@ -335,17 +368,17 @@
             pltpu.VMEM((tasks, 2, EARLY, quarter // 2), BF16),
             pltpu.VMEM((tasks, 2, 4, EARLY, quarter // 2), BF16),
             dma((11,)),
-            dma((tasks, 11)),
+            dma((SLOTS, 11)),
             dma,
             dma((2 * layers, 5)),
-            dma((2,)),
+            dma((3, PARTS)),
+            dma((3,)),
             dma((2 * layers,)),
-            dma((1,)),
         ],
         compiler_params=pltpu.CompilerParams(
-            collective_id=0, has_side_effects=True, vmem_limit_bytes=67043328
+            collective_id=0, has_side_effects=True, vmem_limit_bytes=50 << 20
         ),
-    )(features, jnp.swapaxes(v_weight, 1, 2), u_weight, cross_bias)
+    )(*arguments)
 
 
 def solution(mesh):

time: 146 us -> 132 us (0.904)
  Pallas kernels: 142 us -> 131 us
  local copies, waits for them, and re-layouts: 3.08 us -> 1.32 us
    pallas_call x1, Pallas kernels: 142 us -> 131 us  [local(): pl.pallas_call(kernel, out_shape=jax.ShapeDtypeStruct(features.shape, BF1...]
    unnamed x1, local copies, waits for them, and re-layouts: 3.08 us -> 1.32 us
where the time goes in v5:
time: 132 us
  Pallas kernels  131 us (99%)
  local copies, waits for them, and re-layouts  1.32 us (1%)
    pallas_call x1, Pallas kernels, local(): pl.pallas_call(kernel, out_shape=jax.ShapeDtypeStruct(features.shape, BF1...  131 us

profile of v5, /device:TPU:0, one launch (start us, length us, event | category | flops | bytes accessed | tf_op | source)
XLA Modules:
  0.0 131.9 jit_solution(14038319131579972918)
XLA Ops:
  0.0 130.6 %shard_map.46 = bf16[1024,1024]{1,0:T(8,128)(2,1)S(1)} custom-call(bf16[1024,1024]{1,0:T(8,128)(2,1)} %f_hbm.1, bf16[3,64,1024]{2,1,0:T(8,128)(2,1)} %bitcast.1, bf16[3,64,1024]{2,1,0:T(8,128)(2,1)} %u_hbm.1, f32[3,1024]{1,0:T(4,128)} %b_hbm.1), custom_call_target="tpu_custom_call" | custom-call | tf_op jit(solution)/shard_map/pallas_call | solution.py:346
  130.6 1.3 %copy.6 = bf16[1024,1024]{1,0:T(8,128)(2,1)} copy(bf16[1024,1024]{1,0:T(8,128)(2,1)S(1)} %shard_map.46) | data formatting | bytes 4194304

commit v6 on v5

--- a/solution.py
+++ b/solution.py
@@ -12,10 +12,11 @@
 CHUNKS = 8
 LAG = (0, 1, 2, 3, 4, 5, 7)
 WLAG = (0, 2, 4, 6, 8)
-EARLY = 48
-UPPER_A, UPPER_B = 32, 48
+EARLY = 64
+UPPER_A, UPPER_B = 32, 32
 SLOTS = 8
 PARTS = 4
+DIRECT = 2
 
 
 def kernel(
@@ -23,7 +24,8 @@
     features, w_full, carried, bias,
     part_b, far_b, mid_b, near_b, sum_b, across_b, rank_b,
     part_a, across_a, sum_a, far_a, mid_a, near_a, rank_a,
-    ss, rs, wss, wrs, v0s, in_sem, own_sem,
+    part_d, from_d, sum_d, across_d, rank_d,
+    ss, rs, wss, wrs, v0s, in_sem, own_sem, sd, rd,
 ):
     layers = v_hbm.shape[0]
     matrices = 2 * layers
@@ -44,11 +46,11 @@
     def at(y_hi=y_hi, z=z, core=core, y_lo=y_lo, x=x):
         return ((y_hi * 4 + z) * 2 + core, y_lo * 4 + x)
 
-    right, left, across = at(x=xr), at(x=xl), at(y_lo=1 - y_lo)
+    right, left, opposite, across = at(x=xr), at(x=xl), at(x=xo), at(y_lo=1 - y_lo)
     z_right, z_left, y_far, partner = at(z=zr), at(z=zl), at(y_hi=1 - y_hi), at(core=1 - core)
 
     barrier = pltpu.get_barrier_semaphore()
-    for device in (right, left, across, z_right, z_left, y_far, partner):
+    for device in (right, left, opposite, across, z_right, z_left, y_far, partner):
         pl.semaphore_signal(barrier, inc=1, device_id=device, device_id_type=MESH)
 
     def send(src, dst, send_sem, recv_sem, device):
@@ -201,61 +203,18 @@
     def chunk_rows(chunk):
         return pl.ds(pl.multiple_of(chunk * rows, rows), rows)
 
-    def stage_0(t):
+    def down(t):
         layer, chunk = t // CHUNKS, lax.rem(t, CHUNKS)
         for q in range(4):
-            piece_q = lax.dot_general(
+            yield q, lax.dot_general(
                 carried[chunk],
                 w_full[2 * layer, q * quarter : (q + 1) * quarter, :],
                 (((1,), (1,)), ((), ())),
                 preferred_element_type=F32,
             ).astype(BF16)
-            part_b[t, q] = piece_q[:late]
-            part_a[t, 0, q] = piece_q[late:, : quarter // 2]
-            part_a[t, 1, q] = piece_q[late:, quarter // 2 :]
-        over_y(t, part_a.at[t, 1 - y_lo], across_a.at[t], 9)
-        ways(t)[0][0]()
-
-    def stage_1(t):
-        late_ways, early_ways = ways(t)
-        await_recv(t, 9, across_a)
-        sum_a[t] = (part_a[t, y_lo].astype(F32) + across_a[t].astype(F32)).astype(BF16)
-        early_ways[0]()
-        late_ways[1]()
-
-    def stage_2(t):
-        late_ways, early_ways = ways(t)
-        early_ways[1]()
-        sum_b[t] = late_ways[2]()
-        over_y(t, sum_b.at[t], across_b.at[t], 8)
-
-    def stage_3(t):
-        late_ways, early_ways = ways(t)
-        rank_a[t, y_lo, x] = early_ways[2]()
-        early_ways[3]()
-        await_recv(t, 8, across_b)
-        rank_b[t, x] = (sum_b[t].astype(F32) + across_b[t].astype(F32)).astype(BF16)
-        late_ways[3]()
-
-    def stage_4(t):
-        late_ways, early_ways = ways(t)
-        early_ways[4]()
-        late_ways[4]()
-
-    def stage_5(t):
-        await_recv(t, 7, far_a)
-        over_y(t, rank_a.at[t, y_lo], rank_a.at[t, y_lo], 10)
-
-    def stage_6(t):
+
+    def up(t, lhs):
         layer, chunk = t // CHUNKS, lax.rem(t, CHUNKS)
-        await_recv(t, 3, far_b)
-        await_recv(t, 10, across_a)
-        lhs = [
-            jnp.concatenate(
-                [rank_b[t, q], jnp.concatenate([rank_a[t, 0, q], rank_a[t, 1, q]], axis=1)], axis=0
-            )
-            for q in range(4)
-        ]
         for j in range(4):
             columns = slice(j * depth // 4, (j + 1) * depth // 4)
             total = bias[pl.ds(layer, 1), columns]
@@ -265,16 +224,109 @@
                     w_full[2 * layer + 1, q * quarter : (q + 1) * quarter, columns],
                     preferred_element_type=F32,
                 )
-            new = (
+            carried[chunk, :, columns] = (
                 features[chunk_rows(chunk), columns].astype(F32) * total + carried[chunk, :, columns].astype(F32)
             ).astype(BF16)
-            carried[chunk, :, columns] = new
-
-            @pl.when(layer == layers - 1)
-            def _(columns=columns, new=new):
-                out_ref[chunk_rows(chunk), columns] = new
-
-    stages = (stage_0, stage_1, stage_2, stage_3, stage_4, stage_5, stage_6)
+
+        @pl.when(layer == layers - 1)
+        def _():
+            out_ref[chunk_rows(chunk), :] = carried[chunk]
+
+    def stage_0(t):
+        for q, value in down(t):
+            part_b[t, q] = value[:late]
+            part_a[t, 0, q] = value[late:, : quarter // 2]
+            part_a[t, 1, q] = value[late:, quarter // 2 :]
+        over_y(t, part_a.at[t, 1 - y_lo], across_a.at[t], 9)
+        ways(t)[0][0]()
+
+    def stage_1(t):
+        late_ways, early_ways = ways(t)
+        await_recv(t, 9, across_a)
+        sum_a[t] = (part_a[t, y_lo].astype(F32) + across_a[t].astype(F32)).astype(BF16)
+        early_ways[0]()
+        late_ways[1]()
+
+    def stage_2(t):
+        late_ways, early_ways = ways(t)
+        early_ways[1]()
+        sum_b[t] = late_ways[2]()
+        over_y(t, sum_b.at[t], across_b.at[t], 8)
+
+    def stage_3(t):
+        late_ways, early_ways = ways(t)
+        rank_a[t, y_lo, x] = early_ways[2]()
+        early_ways[3]()
+        await_recv(t, 8, across_b)
+        rank_b[t, x] = (sum_b[t].astype(F32) + across_b[t].astype(F32)).astype(BF16)
+        late_ways[3]()
+
+    def stage_4(t):
+        late_ways, early_ways = ways(t)
+        early_ways[4]()
+        late_ways[4]()
+
+    def stage_5(t):
+        await_recv(t, 7, far_a)
+        over_y(t, rank_a.at[t, y_lo], rank_a.at[t, y_lo], 10)
+
+    def stage_6(t):
+        await_recv(t, 3, far_b)
+        await_recv(t, 10, across_a)
+        up(t, [
+            jnp.concatenate(
+                [rank_b[t, q], jnp.concatenate([rank_a[t, 0, q], rank_a[t, 1, q]], axis=1)], axis=0
+            )
+            for q in range(4)
+        ])
+
+    def await_direct(n, number, size):
+        send(size, size, sd.at[0], rd.at[n, number], right).wait_recv()
+
+    def direct_0(t):
+        n = t - direct_from
+        for q, value in down(t):
+            part_d[n, q] = value
+        start([
+            send(part_d.at[n, xo], from_d.at[n, 2], sd.at[0], rd.at[n, 0], opposite),
+            send(part_d.at[n, xr], from_d.at[n, 0], sd.at[0], rd.at[n, 0], right),
+            send(part_d.at[n, xl], from_d.at[n, 1], sd.at[0], rd.at[n, 0], left),
+        ])
+
+    def direct_1(t):
+        n = t - direct_from
+        await_direct(n, 0, from_d.at[n])
+        sum_d[n] = (
+            part_d[n, x].astype(F32)
+            + from_d[n, 0].astype(F32)
+            + from_d[n, 1].astype(F32)
+            + from_d[n, 2].astype(F32)
+        ).astype(BF16)
+        send(sum_d.at[n], across_d.at[n], sd.at[1], rd.at[n, 1], across).start()
+
+    def direct_2(t):
+        n = t - direct_from
+        await_direct(n, 1, across_d.at[n])
+        rank_d[n, x] = (sum_d[n].astype(F32) + across_d[n].astype(F32)).astype(BF16)
+        start([
+            send(rank_d.at[n, x], rank_d.at[n, x], sd.at[2], rd.at[n, 2], device)
+            for device in (opposite, right, left)
+        ])
+
+    def direct_3(t):
+        n = t - direct_from
+        await_direct(n, 2, from_d.at[n])
+        up(t, [rank_d[n, q] for q in range(4)])
+
+    direct_from = tasks - DIRECT
+    steps = [
+        (stage_0, "s0", LAG[0], 0, direct_from), (direct_0, "d0", 0, direct_from, tasks),
+        (stage_1, "s1", LAG[1], 0, direct_from), (direct_1, "d1", 1, direct_from, tasks),
+        (stage_2, "s2", LAG[2], 0, direct_from), (direct_2, "d2", 2, direct_from, tasks),
+        (stage_3, "s3", LAG[3], 0, direct_from), (stage_4, "s4", LAG[4], 0, direct_from),
+        (stage_5, "s5", LAG[5], 0, direct_from), (stage_6, "s6", LAG[6], 0, direct_from),
+        (direct_3, "d3", 3, direct_from, tasks),
+    ]
 
     for matrix in range(matrices):
         own_piece(matrix).start()
@@ -284,7 +336,7 @@
     ]
     start(fetches)
     with jax.named_scope("barrier"):
-        pl.semaphore_wait(barrier, 7)
+        pl.semaphore_wait(barrier, 8)
     with jax.named_scope("fetch"):
         for matrix in range(matrices):
             own_piece(matrix).wait()
@@ -305,16 +357,16 @@
             with jax.named_scope(f"w{number}"):
                 weight_stages[number](matrix)
 
-    @pl.loop(0, tasks + LAG[6])
+    @pl.loop(0, max(direct_from + LAG[6], tasks + 3))
     def _(i):
         weights_at(i, 4)
-        for number in range(7):
-            t = i - LAG[number]
-
-            @pl.when(jnp.logical_and(t >= 0, t < tasks))
-            def _(number=number, t=t):
-                with jax.named_scope(f"s{number}"):
-                    stages[number](t)
+        for stage, name, lag, first, end in steps:
+            t = i - lag
+
+            @pl.when(jnp.logical_and(t >= first, t < end))
+            def _(stage=stage, name=name, t=t):
+                with jax.named_scope(name):
+                    stage(t)
 
         for number in range(4):
             weights_at(i, number)
@@ -325,6 +377,8 @@
         )
         for number, size in enumerate(sent):
             send(size, size, ss.at[number], rs.at[0, 0], right).wait_send()
+        for number, size in enumerate((from_d, across_d, from_d)):
+            send(size, size, sd.at[number], rd.at[0, 0], right).wait_send()
         for matrix in range(matrices):
             place = w_full.at[matrix, pl.ds(0, weight_sends * share), :]
             send(place, place, wss, wrs.at[0, 0], right).wait_send()
@@ -336,7 +390,7 @@
     rows = features.shape[0] // CHUNKS
     late = rows - EARLY
     quarter = rank // 4
-    tasks = layers * CHUNKS
+    tasks = layers * CHUNKS - DIRECT
     dma = pltpu.SemaphoreType.DMA
     anywhere = pl.BlockSpec(memory_space=pltpu.HBM)
     arguments = [
@@ -367,6 +421,11 @@
             pltpu.VMEM((tasks, EARLY, quarter // 2), BF16),
             pltpu.VMEM((tasks, 2, EARLY, quarter // 2), BF16),
             pltpu.VMEM((tasks, 2, 4, EARLY, quarter // 2), BF16),
+            pltpu.VMEM((DIRECT, 4, rows, quarter), BF16),
+            pltpu.VMEM((DIRECT, 3, rows, quarter), BF16),
+            pltpu.VMEM((DIRECT, rows, quarter), BF16),
+            pltpu.VMEM((DIRECT, rows, quarter), BF16),
+            pltpu.VMEM((DIRECT, 4, rows, quarter), BF16),
             dma((11,)),
             dma((SLOTS, 11)),
             dma,
@@ -374,6 +433,8 @@
             dma((3, PARTS)),
             dma((3,)),
             dma((2 * layers,)),
+            dma((3,)),
+            dma((DIRECT, 3)),
         ],
         compiler_params=pltpu.CompilerParams(
             collective_id=0, has_side_effects=True, vmem_limit_bytes=50 << 20

time: 132 us -> 125 us (0.947)
  Pallas kernels: 131 us -> 123 us
    pallas_call x1, Pallas kernels: 131 us -> 123 us  [local(): pl.pallas_call(kernel, out_shape=jax.ShapeDtypeStruct(features.shape, BF1...]
where the time goes in v6:
time: 125 us
  Pallas kernels  123 us (98%)
  local copies, waits for them, and re-layouts  1.32 us (1%)
    pallas_call x1, Pallas kernels, local(): pl.pallas_call(kernel, out_shape=jax.ShapeDtypeStruct(features.shape, BF1...  123 us

profile of v6, /device:TPU:0, one launch (start us, length us, event | category | flops | bytes accessed | tf_op | source)
XLA Modules:
  0.0 124.6 jit_solution(2765198462856426686)
XLA Ops:
  0.0 123.2 %shard_map.46 = bf16[1024,1024]{1,0:T(8,128)(2,1)S(1)} custom-call(bf16[1024,1024]{1,0:T(8,128)(2,1)} %f_hbm.1, bf16[3,64,1024]{2,1,0:T(8,128)(2,1)} %bitcast.1, bf16[3,64,1024]{2,1,0:T(8,128)(2,1)} %u_hbm.1, f32[3,1024]{1,0:T(4,128)} %b_hbm.1), custom_call_target="tpu_custom_call" | custom-call | tf_op jit(solution)/shard_map/pallas_call | solution.py:400
  123.2 1.3 %copy.6 = bf16[1024,1024]{1,0:T(8,128)(2,1)} copy(bf16[1024,1024]{1,0:T(8,128)(2,1)S(1)} %shard_map.46) | data formatting | bytes 4194304

commit v7 on v6

--- a/solution.py
+++ b/solution.py
@@ -10,13 +10,16 @@
 F32 = jnp.float32
 
 CHUNKS = 8
-LAG = (0, 1, 2, 3, 4, 5, 7)
-WLAG = (0, 2, 4, 6, 8)
+LAGS = {"a1": 1, "a2": 2, "a3": 3, "a4": 4, "a5": 5, "b1": 1, "b2": 2, "b3": 3, "b4": 4, "up": 7}
+ORDER = ("down", "a1", "b1", "a2", "b2", "a3", "b3", "a4", "b4", "a5", "up")
+WLAG = (0, 3, 5, 8)
+WFIRST = -1
 EARLY = 64
 UPPER_A, UPPER_B = 32, 32
 SLOTS = 8
 PARTS = 4
 DIRECT = 2
+DLAG = (0, 1, 2, 5)
 
 
 def kernel(
@@ -83,28 +86,26 @@
 
     def weights_0(matrix):
         start([move(matrix, own, 1, z_right), move(matrix, own, 1, z_left), move(matrix, own, 4, partner)])
+        arrived(matrix, 0, 1)
+        start([move(matrix, other + z, 2, z_right), move(matrix, other + z, 2, z_left),
+               move(matrix, other + z, 4, partner)])
 
     def weights_1(matrix):
         arrived(matrix, 1, 2)
         start([move(matrix, same + zl, 3, z_right), move(matrix, same + zl, 4, partner),
                move(matrix, same + zr, 4, partner)])
-        arrived(matrix, 0, 1)
-        start([move(matrix, other + z, 2, z_right), move(matrix, other + z, 2, z_left),
-               move(matrix, other + z, 4, partner)])
-
-    def weights_2(matrix):
         arrived(matrix, 2, 2)
         start([move(matrix, other + zr, 3, z_left), move(matrix, other + zl, 4, partner),
                move(matrix, other + zr, 4, partner)])
 
-    def weights_3(matrix):
+    def weights_2(matrix):
         arrived(matrix, 3, 2)
         start([move(matrix, same + zo, 4, partner), move(matrix, other + zo, 4, partner)])
 
-    def weights_4(matrix):
+    def weights_3(matrix):
         arrived(matrix, 4, 8)
 
-    weight_stages = (weights_0, weights_1, weights_2, weights_3, weights_4)
+    weight_stages = (weights_0, weights_1, weights_2, weights_3)
     weight_sends = 4 + 6 + 3 + 2
 
     def down_0():
@@ -240,35 +241,40 @@
         over_y(t, part_a.at[t, 1 - y_lo], across_a.at[t], 9)
         ways(t)[0][0]()
 
-    def stage_1(t):
-        late_ways, early_ways = ways(t)
+    def early_1(t):
         await_recv(t, 9, across_a)
         sum_a[t] = (part_a[t, y_lo].astype(F32) + across_a[t].astype(F32)).astype(BF16)
-        early_ways[0]()
-        late_ways[1]()
-
-    def stage_2(t):
-        late_ways, early_ways = ways(t)
-        early_ways[1]()
-        sum_b[t] = late_ways[2]()
-        over_y(t, sum_b.at[t], across_b.at[t], 8)
-
-    def stage_3(t):
-        late_ways, early_ways = ways(t)
+        ways(t)[1][0]()
+
+    def early_2(t):
+        ways(t)[1][1]()
+
+    def early_3(t):
+        early_ways = ways(t)[1]
         rank_a[t, y_lo, x] = early_ways[2]()
         early_ways[3]()
+
+    def early_4(t):
+        ways(t)[1][4]()
+
+    def early_5(t):
+        await_recv(t, 7, far_a)
+        over_y(t, rank_a.at[t, y_lo], rank_a.at[t, y_lo], 10)
+
+    def late_1(t):
+        ways(t)[0][1]()
+
+    def late_2(t):
+        sum_b[t] = ways(t)[0][2]()
+        over_y(t, sum_b.at[t], across_b.at[t], 8)
+
+    def late_3(t):
         await_recv(t, 8, across_b)
         rank_b[t, x] = (sum_b[t].astype(F32) + across_b[t].astype(F32)).astype(BF16)
-        late_ways[3]()
-
-    def stage_4(t):
-        late_ways, early_ways = ways(t)
-        early_ways[4]()
-        late_ways[4]()
-
-    def stage_5(t):
-        await_recv(t, 7, far_a)
-        over_y(t, rank_a.at[t, y_lo], rank_a.at[t, y_lo], 10)
+        ways(t)[0][3]()
+
+    def late_4(t):
+        ways(t)[0][4]()
 
     def stage_6(t):
         await_recv(t, 3, far_b)
@@ -319,14 +325,18 @@
         up(t, [rank_d[n, q] for q in range(4)])
 
     direct_from = tasks - DIRECT
-    steps = [
-        (stage_0, "s0", LAG[0], 0, direct_from), (direct_0, "d0", 0, direct_from, tasks),
-        (stage_1, "s1", LAG[1], 0, direct_from), (direct_1, "d1", 1, direct_from, tasks),
-        (stage_2, "s2", LAG[2], 0, direct_from), (direct_2, "d2", 2, direct_from, tasks),
-        (stage_3, "s3", LAG[3], 0, direct_from), (stage_4, "s4", LAG[4], 0, direct_from),
-        (stage_5, "s5", LAG[5], 0, direct_from), (stage_6, "s6", LAG[6], 0, direct_from),
-        (direct_3, "d3", 3, direct_from, tasks),
-    ]
+    normal = {
+        "a1": early_1, "a2": early_2, "a3": early_3, "a4": early_4, "a5": early_5,
+        "b1": late_1, "b2": late_2, "b3": late_3, "b4": late_4, "up": stage_6,
+    }
+    steps = []
+    for name in ORDER:
+        if name == "down":
+            steps += [(stage_0, name, 0, 0, direct_from), (direct_0, "d0", 0, direct_from, tasks)]
+        else:
+            steps.append((normal[name], name, LAGS[name], 0, direct_from))
+    for stage, number in ((direct_1, 1), (direct_2, 2), (direct_3, 3)):
+        steps.append((stage, f"d{number}", DLAG[number], direct_from, tasks))
 
     for matrix in range(matrices):
         own_piece(matrix).start()
@@ -348,7 +358,7 @@
 
     def weights_at(i, number):
         turn = i - WLAG[number]
-        first = turn == -WLAG[1]
+        first = turn == WFIRST
         matrix = jnp.where(first, 1, turn // 4 + 2)
         regular = jnp.logical_and(jnp.logical_and(turn >= 0, lax.rem(turn, 4) == 0), matrix < matrices)
 
@@ -357,9 +367,9 @@
             with jax.named_scope(f"w{number}"):
                 weight_stages[number](matrix)
 
-    @pl.loop(0, max(direct_from + LAG[6], tasks + 3))
+    @pl.loop(0, max(direct_from + LAGS["up"], tasks + DLAG[3]))
     def _(i):
-        weights_at(i, 4)
+        weights_at(i, 3)
         for stage, name, lag, first, end in steps:
             t = i - lag
 
@@ -368,7 +378,7 @@
                 with jax.named_scope(name):
                     stage(t)
 
-        for number in range(4):
+        for number in range(3):
             weights_at(i, number)
 
     with jax.named_scope("end"):

time: 125 us -> 122 us (0.976)
  Pallas kernels: 123 us -> 120 us
    pallas_call x1, Pallas kernels: 123 us -> 120 us  [local(): pl.pallas_call(kernel, out_shape=jax.ShapeDtypeStruct(features.shape, BF1...]
where the time goes in v7:
time: 122 us
  Pallas kernels  120 us (98%)
  local copies, waits for them, and re-layouts  1.32 us (1%)
    pallas_call x1, Pallas kernels, local(): pl.pallas_call(kernel, out_shape=jax.ShapeDtypeStruct(features.shape, BF1...  120 us

profile of v7, /device:TPU:0, one launch (start us, length us, event | category | flops | bytes accessed | tf_op | source)
XLA Modules:
  0.0 121.6 jit_solution(8405991352132345373)
XLA Ops:
  0.0 120.3 %shard_map.46 = bf16[1024,1024]{1,0:T(8,128)(2,1)S(1)} custom-call(bf16[1024,1024]{1,0:T(8,128)(2,1)} %f_hbm.1, bf16[3,64,1024]{2,1,0:T(8,128)(2,1)} %bitcast.1, bf16[3,64,1024]{2,1,0:T(8,128)(2,1)} %u_hbm.1, f32[3,1024]{1,0:T(4,128)} %b_hbm.1), custom_call_target="tpu_custom_call" | custom-call | tf_op jit(solution)/shard_map/pallas_call | solution.py:410
  120.3 1.3 %copy.6 = bf16[1024,1024]{1,0:T(8,128)(2,1)} copy(bf16[1024,1024]{1,0:T(8,128)(2,1)S(1)} %shard_map.46) | data formatting | bytes 4194304

commit v8 on v7

--- a/solution.py
+++ b/solution.py
@@ -10,23 +10,25 @@
 F32 = jnp.float32
 
 CHUNKS = 8
-LAGS = {"a1": 1, "a2": 2, "a3": 3, "a4": 4, "a5": 5, "b1": 1, "b2": 2, "b3": 3, "b4": 4, "up": 7}
-ORDER = ("down", "a1", "b1", "a2", "b2", "a3", "b3", "a4", "b4", "a5", "up")
+LAGS = {"a1": 2, "a2": 3, "a3": 4, "a4": 5, "b1": 1, "b2": 2, "b3": 3, "b4": 5, "up": 7}
+ORDER = ("down", "a1", "b1", "a2", "b2", "a3", "b3", "a4", "b4", "up")
 WLAG = (0, 3, 5, 8)
 WFIRST = -1
-EARLY = 64
-UPPER_A, UPPER_B = 32, 32
+EARLY = 56
+UPPER_A, UPPER_B = 32, 40
 SLOTS = 8
 PARTS = 4
 DIRECT = 2
-DLAG = (0, 1, 2, 5)
+SOON = 1
+EAGER = 0
+DLAG = (0, 1, 2, 4)
 
 
 def kernel(
     f_hbm, v_hbm, u_hbm, b_hbm, out_ref,
     features, w_full, carried, bias,
     part_b, far_b, mid_b, near_b, sum_b, across_b, rank_b,
-    part_a, across_a, sum_a, far_a, mid_a, near_a, rank_a,
+    part_a, across_a, sum_a, far_a, near_a, rank_a,
     part_d, from_d, sum_d, across_d, rank_d,
     ss, rs, wss, wrs, v0s, in_sem, own_sem, sd, rd,
 ):
@@ -186,13 +188,42 @@
 
         return hop_1, hop_2, total, share_1, share_2
 
+    def straight(t, part, far, near, rank, first):
+        def hop():
+            start([
+                send(part(xo), far.at[t], ss.at[first + 1], rs.at[lax.rem(t, SLOTS), first], opposite),
+                send(part(xr), near.at[t, 0], ss.at[first], rs.at[lax.rem(t, SLOTS), first + 1], right),
+                send(part(xl), near.at[t, 1], ss.at[first], rs.at[lax.rem(t, SLOTS), first + 1], left),
+            ])
+
+        def total():
+            await_recv(t, first, far)
+            await_recv(t, first + 1, near)
+            return (
+                part(x)[...].astype(F32) + near[t, 0].astype(F32) + near[t, 1].astype(F32) + far[t].astype(F32)
+            ).astype(BF16)
+
+        upper, lower = pl.ds(0, UPPER_A), pl.ds(UPPER_A, EARLY - UPPER_A)
+
+        def share_1():
+            start([
+                send(rank(x), rank(x), ss.at[first + 2], rs.at[lax.rem(t, SLOTS), first + 2], right),
+                send(rank(x), rank(x), ss.at[first + 2], rs.at[lax.rem(t, SLOTS), first + 2], left),
+            ])
+
+        def share_2():
+            await_recv(t, first + 2, near)
+            for q, part_of, device in ((xl, lower, right), (xr, upper, left)):
+                place = rank(q).at[part_of]
+                send(place, place, ss.at[first + 3], rs.at[lax.rem(t, SLOTS), first + 3], device).start()
+
+        return hop, total, share_1, share_2
+
     def ways(t):
         late_ways = to_right_and_left(
             t, late, UPPER_B, lambda q: part_b.at[t, q], far_b, mid_b, near_b, lambda q: rank_b.at[t, q], 0
         )
-        early_ways = to_right_and_left(
-            t, EARLY, UPPER_A, lambda q: sum_a.at[t, q], far_a, mid_a, near_a, lambda q: rank_a.at[t, y_lo, q], 4
-        )
+        early_ways = straight(t, lambda q: sum_a.at[t, q], far_a, near_a, lambda q: rank_a.at[t, y_lo, q], 4)
         return late_ways, early_ways
 
     def over_y(t, src, dst, number):
@@ -247,17 +278,14 @@
         ways(t)[1][0]()
 
     def early_2(t):
-        ways(t)[1][1]()
+        early_ways = ways(t)[1]
+        rank_a[t, y_lo, x] = early_ways[1]()
+        early_ways[2]()
 
     def early_3(t):
-        early_ways = ways(t)[1]
-        rank_a[t, y_lo, x] = early_ways[2]()
-        early_ways[3]()
+        ways(t)[1][3]()
 
     def early_4(t):
-        ways(t)[1][4]()
-
-    def early_5(t):
         await_recv(t, 7, far_a)
         over_y(t, rank_a.at[t, y_lo], rank_a.at[t, y_lo], 10)
 
@@ -326,16 +354,19 @@
 
     direct_from = tasks - DIRECT
     normal = {
-        "a1": early_1, "a2": early_2, "a3": early_3, "a4": early_4, "a5": early_5,
+        "a1": early_1, "a2": early_2, "a3": early_3, "a4": early_4,
         "b1": late_1, "b2": late_2, "b3": late_3, "b4": late_4, "up": stage_6,
     }
     steps = []
     for name in ORDER:
         if name == "down":
-            steps += [(stage_0, name, 0, 0, direct_from), (direct_0, "d0", 0, direct_from, tasks)]
+            steps.append((stage_0, name, 0, 0, direct_from))
+        elif name == "up":
+            steps.append((stage_6, name, LAGS[name], 0, direct_from - SOON))
+            steps.append((stage_6, name, LAGS["up"] - EAGER, direct_from - SOON, direct_from))
         else:
             steps.append((normal[name], name, LAGS[name], 0, direct_from))
-    for stage, number in ((direct_1, 1), (direct_2, 2), (direct_3, 3)):
+    for number, stage in ((0, direct_0), (1, direct_1), (2, direct_2), (3, direct_3)):
         steps.append((stage, f"d{number}", DLAG[number], direct_from, tasks))
 
     for matrix in range(matrices):
@@ -367,7 +398,7 @@
             with jax.named_scope(f"w{number}"):
                 weight_stages[number](matrix)
 
-    @pl.loop(0, max(direct_from + LAGS["up"], tasks + DLAG[3]))
+    @pl.loop(0, max(direct_from - SOON + LAGS["up"], direct_from + LAGS["up"] - EAGER, tasks + DLAG[3]))
     def _(i):
         weights_at(i, 3)
         for stage, name, lag, first, end in steps:
@@ -428,7 +459,6 @@
             pltpu.VMEM((tasks, 4, EARLY, quarter // 2), BF16),
             pltpu.VMEM((tasks, 4, EARLY, quarter // 2), BF16),
             pltpu.VMEM((tasks, EARLY, quarter // 2), BF16),
-            pltpu.VMEM((tasks, EARLY, quarter // 2), BF16),
             pltpu.VMEM((tasks, 2, EARLY, quarter // 2), BF16),
             pltpu.VMEM((tasks, 2, 4, EARLY, quarter // 2), BF16),
             pltpu.VMEM((DIRECT, 4, rows, quarter), BF16),

time: 122 us -> 120 us (0.984)
  Pallas kernels: 120 us -> 118 us
    pallas_call x1, Pallas kernels: 120 us -> 118 us  [local(): pl.pallas_call(kernel, out_shape=jax.ShapeDtypeStruct(features.shape, BF1...]
where the time goes in v8:
time: 120 us
  Pallas kernels  118 us (98%)
  local copies, waits for them, and re-layouts  1.32 us (1%)
    pallas_call x1, Pallas kernels, local(): pl.pallas_call(kernel, out_shape=jax.ShapeDtypeStruct(features.shape, BF1...  118 us

profile of v8, /device:TPU:0, one launch (start us, length us, event | category | flops | bytes accessed | tf_op | source)
XLA Modules:
  0.0 119.8 jit_solution(18361531746682959554)
XLA Ops:
  0.0 118.4 %shard_map.46 = bf16[1024,1024]{1,0:T(8,128)(2,1)S(1)} custom-call(bf16[1024,1024]{1,0:T(8,128)(2,1)} %f_hbm.1, bf16[3,64,1024]{2,1,0:T(8,128)(2,1)} %bitcast.1, bf16[3,64,1024]{2,1,0:T(8,128)(2,1)} %u_hbm.1, f32[3,1024]{1,0:T(4,128)} %b_hbm.1), custom_call_target="tpu_custom_call" | custom-call | tf_op jit(solution)/shard_map/pallas_call | solution.py:441
  118.4 1.3 %copy.6 = bf16[1024,1024]{1,0:T(8,128)(2,1)} copy(bf16[1024,1024]{1,0:T(8,128)(2,1)S(1)} %shard_map.46) | data formatting | bytes 4194304

commit v9 on v8

--- a/solution.py
+++ b/solution.py
@@ -11,17 +11,17 @@
 
 CHUNKS = 8
 LAGS = {"a1": 2, "a2": 3, "a3": 4, "a4": 5, "b1": 1, "b2": 2, "b3": 3, "b4": 5, "up": 7}
-ORDER = ("down", "a1", "b1", "a2", "b2", "a3", "b3", "a4", "b4", "up")
+ORDER = ("down", "a1", "a2", "b1", "b2", "a3", "b3", "a4", "b4", "up")
 WLAG = (0, 3, 5, 8)
 WFIRST = -1
-EARLY = 56
-UPPER_A, UPPER_B = 32, 40
+EARLY = 64
+UPPER_A, UPPER_B = 32, 32
 SLOTS = 8
 PARTS = 4
 DIRECT = 2
 SOON = 1
 EAGER = 0
-DLAG = (0, 1, 2, 4)
+DLAG = (0, 2, 3, 5)
 
 
 def kernel(

time: 120 us -> 119 us (level)
  no operation moved by 1% of the time
where the time goes in v9:
time: 119 us
  Pallas kernels  118 us (99%)
  local copies, waits for them, and re-layouts  1.32 us (1%)
    pallas_call x1, Pallas kernels, local(): pl.pallas_call(kernel, out_shape=jax.ShapeDtypeStruct(features.shape, BF1...  118 us

profile of v9, /device:TPU:0, one launch (start us, length us, event | category | flops | bytes accessed | tf_op | source)
XLA Modules:
  0.0 119.0 jit_solution(8192179434598024272)
XLA Ops:
  0.0 117.6 %shard_map.46 = bf16[1024,1024]{1,0:T(8,128)(2,1)S(1)} custom-call(bf16[1024,1024]{1,0:T(8,128)(2,1)} %f_hbm.1, bf16[3,64,1024]{2,1,0:T(8,128)(2,1)} %bitcast.1, bf16[3,64,1024]{2,1,0:T(8,128)(2,1)} %u_hbm.1, f32[3,1024]{1,0:T(4,128)} %b_hbm.1), custom_call_target="tpu_custom_call" | custom-call | tf_op jit(solution)/shard_map/pallas_call | solution.py:441
  117.6 1.3 %copy.6 = bf16[1024,1024]{1,0:T(8,128)(2,1)} copy(bf16[1024,1024]{1,0:T(8,128)(2,1)S(1)} %shard_map.46) | data formatting | bytes 4194304
